TPU v7x, 32 devices: a whole 2x2x4 slice. The times are simulated.
32 devices in a mesh: gx: 4 (over y, x), gy: 4 (over z), gz: 2 (over core).
Axes of the slice: x: 2, y: 2, z: 4, core: 2. Of those that a mesh axis runs over, the one named last changes fastest.
Arguments:
- positions: float32 [12, 12, 16, 96], P('gx', 'gy', 'gz'), may hold values from 0 to 1
- types: int32 [12, 12, 16, 32], P('gx', 'gy', 'gz'), may hold values from 0 to 2
Outputs:
- forces_energy: float32 [12, 12, 16, 128], P('gx', 'gy', 'gz')
Inputs may be any that keep to these rules, and one draw needn't show every extreme that they name: `types`: 0 marks an empty slot, 1 a copper atom, 2 a nickel atom.
All inputs are finite; a program needn't handle non-finite values.
Results may differ from a plain program's by a relative error of at most 0.0001.
Values sent between devices are 32-bit elements; how exact they have to be, the bound alone decides.
A program may use at most 64 MiB of HBM per device.

v0:
```python
import functools
import math

import jax
import jax.numpy as jnp
from jax import lax
from jax.experimental import pallas as pl
from jax.experimental.pallas import tpu as pltpu
from jax.sharding import PartitionSpec as P

cut_square = 0.9025
density_rate = 3.0
unit = density_rate * math.log2(math.e)
alpha = math.sqrt(unit)
kappa = unit * cut_square
tail = 2.0**-kappa
shift_big = 2.0 * kappa / (cut_square * density_rate)
density_scale = tail / kappa**2
energy_scale = 0.25 * tail**2 / kappa**2
force_scale = -2.0 * tail**2 * density_rate / (kappa**2 * alpha)
slope_scale = -0.5 / tail

AXES = ("gx", "gy", "gz")
DIRECTIONS = [
    (a, b, c)
    for a in (-1, 0, 1)
    for b in (-1, 0, 1)
    for c in (-1, 0, 1)
    if (a, b, c) != (0, 0, 0)
]


def kernel(dims, axis_sizes, pay_ref, out_ref, pad, pad_phi, spread, spread_phi, own, hot, block,
           pair_e, pair_m, pair_q, send_sem, recv_sem, send_phi, recv_phi):
    nx, ny, nz, slots = dims
    lanes = nz * slots
    me = [lax.axis_index(axis) for axis in AXES]

    def peer(direction):
        return {
            axis: lax.rem(place + step + size, size)
            for axis, place, step, size in zip(AXES, me, direction, axis_sizes)
        }

    barrier = pltpu.get_barrier_semaphore()
    for direction in DIRECTIONS:
        pl.semaphore_signal(
            barrier, inc=1, device_id=peer(direction), device_id_type=pl.DeviceIdType.MESH
        )
    pl.semaphore_wait(barrier, len(DIRECTIONS))

    def source_range(step, length):
        return pl.ds(length - 1, 1) if step > 0 else pl.ds(0, 1) if step < 0 else pl.ds(0, length)

    def target_range(step, length):
        return pl.ds(0, 1) if step > 0 else pl.ds(length + 1, 1) if step < 0 else pl.ds(1, length)

    copies = []
    for index, direction in enumerate(DIRECTIONS):
        a, b, c = direction
        zs = source_range(c, nz)
        copy = pltpu.make_async_remote_copy(
            src_ref=pay_ref.at[source_range(a, nx), source_range(b, ny), zs],
            dst_ref=pad.at[target_range(a, nx), target_range(b, ny), 1 - c, zs],
            send_sem=send_sem.at[index],
            recv_sem=recv_sem.at[index],
            device_id=peer(direction),
            device_id_type=pl.DeviceIdType.MESH,
        )
        copy.start()
        copies.append(copy)

    row = lax.broadcasted_iota(jnp.int32, (9 * nz, lanes), 0) % (3 * nz)
    cell = lax.broadcasted_iota(jnp.int32, (9 * nz, lanes), 1) // slots
    for dz in range(3):
        hot[:, dz * lanes : (dz + 1) * lanes] = jnp.where(
            row == cell + (nz - 1 + dz), 1.0, 0.0
        ).astype(jnp.bfloat16)
    block_row = lax.broadcasted_iota(jnp.int32, (lanes, lanes), 0) // slots
    block_col = lax.broadcasted_iota(jnp.int32, (lanes, lanes), 1) // slots
    block[...] = jnp.where(block_row == block_col, 1.0, 0.0).astype(jnp.bfloat16)
    diagonal = (
        lax.broadcasted_iota(jnp.int32, (slots, lanes), 1) % slots
        == lax.broadcasted_iota(jnp.int32, (slots, lanes), 0)
    )

    for x in range(nx):
        for y in range(ny):
            pad[x + 1, y + 1, 1] = pay_ref[x, y]

    for copy in copies:
        copy.wait()

    zrow = lax.broadcasted_iota(jnp.int32, (3 * nz, 4 * slots), 0)
    valid = (zrow >= nz - 1) & (zrow <= 2 * nz)

    def pieces(value):
        high = value.astype(jnp.bfloat16).astype(jnp.float32)
        rest = value - high
        middle = rest.astype(jnp.bfloat16).astype(jnp.float32)
        return high, middle, rest - middle

    def expand(t, carry):
        x, y = t // (ny + 2), t % (ny + 2)
        value = jnp.concatenate([pad[x, y, 0], pad[x, y, 1], pad[x, y, 2]], axis=0)
        value = jnp.where(valid, value, 0.0)
        stacked = jnp.concatenate(pieces(value), axis=0).astype(jnp.bfloat16)
        for dz in range(3):
            spread[x, y, dz] = lax.dot_general(
                stacked,
                hot[:, dz * lanes : (dz + 1) * lanes],
                (((0,), (0,)), ((), ())),
                preferred_element_type=jnp.float32,
            )
        return carry

    lax.fori_loop(0, (nx + 2) * (ny + 2), expand, 0)

    def density(t, carry):
        x, y = t // ny, t % ny
        mine = [
            jnp.sum(
                jnp.where(diagonal, spread[x + 1, y + 1, 1, k * slots : (k + 1) * slots, :], 0.0),
                axis=0,
                keepdims=True,
            )
            for k in range(4)
        ]
        for k in range(4):
            own[t, k : k + 1, :] = mine[k]

        def step(n, sums):
            rho, energy = sums
            a, b = n // 3, n % 3
            px = jnp.broadcast_to(mine[0] - (a - 1).astype(jnp.float32) * alpha, (8, lanes))
            py = jnp.broadcast_to(mine[1] - (b - 1).astype(jnp.float32) * alpha, (8, lanes))
            for dz in range(3):
                pz = jnp.broadcast_to(mine[2] - (dz - 1) * alpha, (8, lanes))
                for r in range(0, slots, 8):
                    dx = spread[x + a, y + b, dz, r : r + 8, :] - px
                    dy = spread[x + a, y + b, dz, slots + r : slots + r + 8, :] - py
                    dd = spread[x + a, y + b, dz, 2 * slots + r : 2 * slots + r + 8, :] - pz
                    wj = spread[x + a, y + b, dz, 3 * slots + r : 3 * slots + r + 8, :]
                    m = jnp.maximum(kappa - (dx * dx + dy * dy + dd * dd), 0.0)
                    e = jnp.exp2(m)
                    em = e * m
                    q = em * wj
                    rho = rho + q * m
                    energy = energy + q * em
                    pair_e[t, n, dz, r : r + 8, :] = e
                    pair_m[t, n, dz, r : r + 8, :] = m
                    pair_q[t, n, dz, r : r + 8, :] = q
            return rho, energy

        zero = jnp.zeros((8, lanes), jnp.float32)
        rho, energy = lax.fori_loop(0, 9, step, (zero, zero))
        w = mine[3]
        rho = jnp.sum(rho, axis=0, keepdims=True) * density_scale - w
        energy = jnp.sum(energy, axis=0, keepdims=True) * (energy_scale * w) - 0.25 * w * w
        root = jnp.sqrt(jnp.maximum(rho, 0.0) + 1.0)
        big = w > 1.3
        ratio = jnp.where(big, 0.875, jnp.where(w > 0.5, 1.0, 0.0))
        a = jnp.where(big, 1.4, jnp.where(w > 0.5, 1.0, 0.0))
        phi = slope_scale * ratio / root
        out_ref[t, 3:4, :] = energy - a * root
        pad_phi[x + 1, y + 1, :, 128 : 128 + lanes] = phi
        return carry

    lax.fori_loop(0, nx * ny, density, 0)

    def lane_source(step):
        return (
            pl.ds(lanes, 128) if step > 0 else pl.ds(128, 128) if step < 0 else pl.ds(128, lanes)
        )

    def lane_target(step):
        return (
            pl.ds(0, 128)
            if step > 0
            else pl.ds(128 + lanes, 128)
            if step < 0
            else pl.ds(128, lanes)
        )

    def inner_source(step, length):
        return pl.ds(length, 1) if step > 0 else pl.ds(1, 1) if step < 0 else pl.ds(1, length)

    copies = []
    for index, direction in enumerate(DIRECTIONS):
        a, b, c = direction
        copy = pltpu.make_async_remote_copy(
            src_ref=pad_phi.at[inner_source(a, nx), inner_source(b, ny), :, lane_source(c)],
            dst_ref=pad_phi.at[target_range(a, nx), target_range(b, ny), :, lane_target(c)],
            send_sem=send_phi.at[index],
            recv_sem=recv_phi.at[index],
            device_id=peer(direction),
            device_id_type=pl.DeviceIdType.MESH,
        )
        copy.start()
        copies.append(copy)
    for copy in copies:
        copy.wait()

    def expand_phi(t, carry):
        x, y = t // (ny + 2), t % (ny + 2)
        value = pad_phi[x, y]
        for dz in range(3):
            start = 128 + (dz - 1) * slots
            part = jnp.where(diagonal, value[:, start : start + lanes], 0.0)
            stacked = jnp.concatenate(pieces(part), axis=0).astype(jnp.bfloat16)
            result = jnp.dot(stacked, block[...], preferred_element_type=jnp.float32)
            spread_phi[x, y, dz] = (
                result[:slots] + result[slots : 2 * slots] + result[2 * slots :]
            )
        return carry

    lax.fori_loop(0, (nx + 2) * (ny + 2), expand_phi, 0)

    def force(t, carry):
        x, y = t // ny, t % ny
        mine = [own[t, k : k + 1, :] for k in range(4)]
        phi = jnp.broadcast_to(pad_phi[x + 1, y + 1, :, 128 : 128 + lanes], (8, lanes))

        def step(n, sums):
            fx, fy, fz = sums
            a, b = n // 3, n % 3
            px = jnp.broadcast_to(mine[0] - (a - 1).astype(jnp.float32) * alpha, (8, lanes))
            py = jnp.broadcast_to(mine[1] - (b - 1).astype(jnp.float32) * alpha, (8, lanes))
            for dz in range(3):
                pz = jnp.broadcast_to(mine[2] - (dz - 1) * alpha, (8, lanes))
                for r in range(0, slots, 8):
                    dx = spread[x + a, y + b, dz, r : r + 8, :] - px
                    dy = spread[x + a, y + b, dz, slots + r : slots + r + 8, :] - py
                    dd = spread[x + a, y + b, dz, 2 * slots + r : 2 * slots + r + 8, :] - pz
                    e = pair_e[t, n, dz, r : r + 8, :]
                    m = pair_m[t, n, dz, r : r + 8, :]
                    q = pair_q[t, n, dz, r : r + 8, :]
                    both = phi + spread_phi[x + a, y + b, dz, r : r + 8, :]
                    v = q * (both * (m + shift_big) + e * (m + 0.5 * shift_big))
                    fx = fx + v * dx
                    fy = fy + v * dy
                    fz = fz + v * dd
            return fx, fy, fz

        zero = jnp.zeros((8, lanes), jnp.float32)
        sums = lax.fori_loop(0, 9, step, (zero, zero, zero))
        scale = force_scale * mine[3]
        for k in range(3):
            out_ref[t, k : k + 1, :] = jnp.sum(sums[k], axis=0, keepdims=True) * scale
        return carry

    lax.fori_loop(0, nx * ny, force, 0)


def body(axis_sizes, positions, types):
    nx, ny, nz, slots = types.shape
    lanes = nz * slots
    weight = jnp.where(types == 1, 1.0, jnp.where(types == 2, 1.6, 0.0)).astype(jnp.float32)
    payload = jnp.concatenate([positions * alpha, weight], axis=3)
    count = len(DIRECTIONS)
    columns = nx * ny
    out = pl.pallas_call(
        functools.partial(kernel, (nx, ny, nz, slots), axis_sizes),
        out_shape=jax.ShapeDtypeStruct((columns, 4, lanes), jnp.float32),
        in_specs=[pl.BlockSpec(memory_space=pltpu.VMEM)],
        out_specs=pl.BlockSpec(memory_space=pltpu.VMEM),
        scratch_shapes=[
            pltpu.VMEM((nx + 2, ny + 2, 3, nz, 4 * slots), jnp.float32),
            pltpu.VMEM((nx + 2, ny + 2, 1, lanes + 256), jnp.float32),
            pltpu.VMEM((nx + 2, ny + 2, 3, 4 * slots, lanes), jnp.float32),
            pltpu.VMEM((nx + 2, ny + 2, 3, slots, lanes), jnp.float32),
            pltpu.VMEM((columns, 8, lanes), jnp.float32),
            pltpu.VMEM((9 * nz, 3 * lanes), jnp.bfloat16),
            pltpu.VMEM((lanes, lanes), jnp.bfloat16),
            pltpu.VMEM((columns, 9, 3, slots, lanes), jnp.float32),
            pltpu.VMEM((columns, 9, 3, slots, lanes), jnp.float32),
            pltpu.VMEM((columns, 9, 3, slots, lanes), jnp.float32),
            pltpu.SemaphoreType.DMA((count,)),
            pltpu.SemaphoreType.DMA((count,)),
            pltpu.SemaphoreType.DMA((count,)),
            pltpu.SemaphoreType.DMA((count,)),
        ],
        compiler_params=pltpu.CompilerParams(
            collective_id=0, has_side_effects=True, vmem_limit_bytes=60 * 1024 * 1024
        ),
    )(payload)
    out = out.reshape(nx, ny, 4, nz, slots).transpose(0, 1, 3, 2, 4)
    return out.reshape(nx, ny, nz, 4 * slots)


def solution(mesh):
    spec = P("gx", "gy", "gz", None)
    sizes = tuple(mesh.shape[axis] for axis in AXES)
    return jax.shard_map(
        functools.partial(body, sizes),
        mesh=mesh,
        in_specs=(spec, spec),
        out_specs=spec,
        check_vma=False,
    )
```

profile of v0, /device:TPU:0, one launch (start us, length us, event | category | flops | bytes accessed | tf_op | source)
XLA Modules:
  0.0 47.2 jit_solution(15573361176364283768)
XLA Ops:
  0.0 0.0 copy-start
  0.0 0.8 %broadcast_multiply_fusion = f32[3,3,8,96]{3,2,1,0:T(8,128)S(1)} fusion(f32[3,3,8,96]{3,2,1,0:T(8,128)} %param.2), kind=kLoop, calls=%fused_computation.2 | loop fusion | flops 6912 | bytes 55296 | tf_op jit(solution)/shard_map/mul | solution.py:259
  0.8 0.0 copy-done
  0.8 0.7 %pad_maximum_fusion.pay_ref = f32[3,3,8,128]{3,2,1,0:T(8,128)} fusion(f32[3,3,8,32]{3,2,1,0:T(8,128)S(1)} %select_select_fusion, f32[3,3,8,96]{3,2,1,0:T(8,128)S(1)} %broadcast_multiply_fusion), kind=kLoop, calls=%fused_computation | loop fusion | flops 9216 | bytes 73728 | tf_op jit(solution)/shard_map/concatenate | solution.py:259
  1.5 44.0 %shard_map.28 = f32[9,4,256]{2,1,0:T(4,128)} custom-call(f32[3,3,8,128]{3,2,1,0:T(8,128)} %pad_maximum_fusion.pay_ref), custom_call_target="tpu_custom_call" | custom-call | tf_op jit(solution)/shard_map/pallas_call | solution.py:262
  45.6 0.9 %reshape.6 = f32[3,3,4,8,32]{4,3,2,1,0:T(8,128)S(1)} reshape(f32[9,4,256]{2,1,0:T(4,128)} %shard_map.28) | data formatting | bytes 73728 | tf_op jit(solution)/shard_map/reshape | solution.py:287
  46.5 0.7 %reshape.7 = f32[3,3,8,128]{3,2,1,0:T(8,128)} reshape(f32[3,3,8,4,32]{4,3,2,1,0:T(4,128)S(1)} %copy.3) | data formatting | bytes 73728 | tf_op jit(solution)/shard_map/reshape | solution.py:288
  (2 shorter events, 0.0 us)
Async XLA Ops:
  0.0 0.8 %copy-start = (s32[3,3,8,32]{3,2,1,0:T(8,128)S(1)}, s32[3,3,8,32]{3,2,1,0:T(8,128)}, u32[]{:S(2)}) copy-start(s32[3,3,8,32]{3,2,1,0:T(8,128)} %param.3) | copy-start | bytes 27652
where the time goes:
time: 47.5 us; the launch traced here: 47.2 us
  Pallas kernels  44 us (93%)
  local copies, waits for them, and re-layouts  1.65 us (3%)
  other arithmetic  1.49 us (3%)
    pallas_call x1, Pallas kernels, body(): pl.pallas_call(functools.partial(kernel, (nx, ny, nz, slots), axis_sizes)...  44 us

commit v1 on v0

v1 whole, which is shorter than its diff:
```python
import functools
import math

import jax
import jax.numpy as jnp
from jax import lax
from jax.experimental import pallas as pl
from jax.experimental.pallas import tpu as pltpu
from jax.sharding import PartitionSpec as P

cut_square = 0.9025
density_rate = 3.0
unit = density_rate * math.log2(math.e)
alpha = math.sqrt(unit)
kappa = unit * cut_square
tail = 2.0**-kappa
shift_big = 2.0 * kappa / (cut_square * density_rate)
density_scale = tail / kappa**2
energy_scale = 0.25 * tail**2 / kappa**2
force_scale = -2.0 * tail**2 * density_rate / (kappa**2 * alpha)
slope_scale = -0.5 / tail

AXES = ("gx", "gy", "gz")
DIRECTIONS = sorted(
    (
        (a, b, c)
        for a in (-1, 0, 1)
        for b in (-1, 0, 1)
        for c in (-1, 0, 1)
        if (a, b, c) != (0, 0, 0)
    ),
    key=lambda d: -(2 * abs(d[0]) + 2 * abs(d[1]) + abs(d[2])),
)
WIDE = 128


def kernel(dims, axis_sizes, pos_ref, typ_ref, out_ref, pos, typ, pad, pad_phi, spread, spread_phi,
           own, acc, acc_force, rows, phi_rows, hot, pair_e, pair_m, pair_q,
           load_sem, send_sem, recv_sem, send_phi, recv_phi):
    nx, ny, nz, slots = dims
    lanes = nz * slots
    base = 8
    me = [lax.axis_index(axis) for axis in AXES]

    def peer(direction):
        return {
            axis: lax.rem(place + step + size, size)
            for axis, place, step, size in zip(AXES, me, direction, axis_sizes)
        }

    barrier = pltpu.get_barrier_semaphore()
    for direction in DIRECTIONS:
        pl.semaphore_signal(
            barrier, inc=1, device_id=peer(direction), device_id_type=pl.DeviceIdType.MESH
        )
    loads = [
        pltpu.make_async_copy(pos_ref, pos, load_sem.at[0]),
        pltpu.make_async_copy(typ_ref, typ, load_sem.at[1]),
    ]
    for load in loads:
        load.start()

    row = lax.broadcasted_iota(jnp.int32, (3 * nz, lanes), 0) % nz
    cell = lax.broadcasted_iota(jnp.int32, (3 * nz, lanes), 1) // slots
    hot[...] = jnp.where(row == cell, 1.0, 0.0).astype(jnp.bfloat16)
    diagonal = (
        lax.broadcasted_iota(jnp.int32, (slots, lanes), 1) % slots
        == lax.broadcasted_iota(jnp.int32, (slots, lanes), 0)
    )
    cell_mask = (
        lax.broadcasted_iota(jnp.int32, (nz, lanes), 1) // slots
        == lax.broadcasted_iota(jnp.int32, (nz, lanes), 0)
    )
    group = lax.broadcasted_iota(jnp.int32, (nz, WIDE), 1) // slots

    for load in loads:
        load.wait()
    for x in range(nx):
        for y in range(ny):
            kind = typ[x, y]
            weight = jnp.where(kind == 1, 1.0, jnp.where(kind == 2, 1.6, 0.0)).astype(jnp.float32)
            pad[x + 1, y + 1, base : base + nz, :] = jnp.concatenate(
                [pos[x, y] * alpha, weight], axis=1
            )

    def pieces(value):
        high = value.astype(jnp.bfloat16).astype(jnp.float32)
        rest = value - high
        middle = rest.astype(jnp.bfloat16).astype(jnp.float32)
        return high, middle, rest - middle

    def spread_out(blocks):
        wide = blocks[0] if len(blocks) == 1 else jnp.concatenate(blocks, axis=1)
        stacked = jnp.concatenate(pieces(wide), axis=0).astype(jnp.bfloat16)
        return lax.dot_general(
            stacked, hot[...], (((0,), (0,)), ((), ())), preferred_element_type=jnp.float32
        )

    def expand(blocks):
        result = spread_out(
            [pad[x, y, base - 1 + dz : base - 1 + dz + nz, :] for x, y, dz in blocks]
        )
        for k, (x, y, dz) in enumerate(blocks):
            spread[x, y, dz] = result[k * WIDE : (k + 1) * WIDE]

    many = WIDE // slots

    def expand_phi(blocks):
        wide = []
        for start in range(0, len(blocks), many):
            part = [
                pad_phi[x, y, base - 1 + dz : base - 1 + dz + nz, :]
                for x, y, dz in blocks[start : start + many]
            ]
            value = part[-1]
            for k in reversed(range(len(part) - 1)):
                value = jnp.where(group == k, part[k], value)
            wide.append(value)
        result = spread_out(wide)
        for k, (x, y, dz) in enumerate(blocks):
            spread_phi[x, y, dz] = result[k * slots : (k + 1) * slots]

    def density(x, y, a, b, layers, sums):
        rho, energy = sums
        t, n = x * ny + y, 3 * a + b
        px = own[t, 0:1, :] - jnp.asarray(a - 1, jnp.float32) * alpha
        py = own[t, 1:2, :] - jnp.asarray(b - 1, jnp.float32) * alpha
        px = jnp.broadcast_to(px, (8, lanes))
        py = jnp.broadcast_to(py, (8, lanes))
        for dz in layers:
            pz = jnp.broadcast_to(own[t, 2:3, :] - (dz - 1) * alpha, (8, lanes))
            for r in range(0, slots, 8):
                dx = spread[x + a, y + b, dz, r : r + 8, :] - px
                dy = spread[x + a, y + b, dz, slots + r : slots + r + 8, :] - py
                dd = spread[x + a, y + b, dz, 2 * slots + r : 2 * slots + r + 8, :] - pz
                wj = spread[x + a, y + b, dz, 3 * slots + r : 3 * slots + r + 8, :]
                m = jnp.maximum(kappa - (dx * dx + dy * dy + dd * dd), 0.0)
                e = jnp.exp2(m)
                em = e * m
                q = em * wj
                rho = rho + q * m
                energy = energy + q * em
                pair_e[t, n, dz, r : r + 8, :] = e
                pair_m[t, n, dz, r : r + 8, :] = m
                pair_q[t, n, dz, r : r + 8, :] = q
        return rho, energy

    def force(x, y, a, b, layers, sums):
        fx, fy, fz = sums
        t, n = x * ny + y, 3 * a + b
        px = own[t, 0:1, :] - jnp.asarray(a - 1, jnp.float32) * alpha
        py = own[t, 1:2, :] - jnp.asarray(b - 1, jnp.float32) * alpha
        px = jnp.broadcast_to(px, (8, lanes))
        py = jnp.broadcast_to(py, (8, lanes))
        phi = jnp.broadcast_to(own[t, 4:5, :], (8, lanes))
        for dz in layers:
            pz = jnp.broadcast_to(own[t, 2:3, :] - (dz - 1) * alpha, (8, lanes))
            for r in range(0, slots, 8):
                dx = spread[x + a, y + b, dz, r : r + 8, :] - px
                dy = spread[x + a, y + b, dz, slots + r : slots + r + 8, :] - py
                dd = spread[x + a, y + b, dz, 2 * slots + r : 2 * slots + r + 8, :] - pz
                e = pair_e[t, n, dz, r : r + 8, :]
                m = pair_m[t, n, dz, r : r + 8, :]
                q = pair_q[t, n, dz, r : r + 8, :]
                both = phi + spread_phi[x + a, y + b, dz, r : r + 8, :]
                v = q * (both * (m + shift_big) + e * (m + 0.5 * shift_big))
                fx = fx + v * dx
                fy = fy + v * dy
                fz = fz + v * dd
        return fx, fy, fz

    def over(function, target, x, y, a_range, b_range, layers, fresh):
        t = x * ny + y
        count = target.shape[1]
        zero = jnp.zeros((8, lanes), jnp.float32)
        sums = tuple(zero if fresh else target[t, k] for k in range(count))

        def along(a, sums):
            return lax.fori_loop(
                b_range[0], b_range[1], lambda b, s: function(x, y, a, b, layers, s), sums
            )

        if isinstance(a_range, int):
            sums = along(a_range, sums)
        else:
            sums = lax.fori_loop(a_range[0], a_range[1], along, sums)
        for k in range(count):
            target[t, k] = sums[k]

    def inside(place, length):
        return jnp.maximum(0, 1 - place), jnp.minimum(3, length + 1 - place)

    def own_pairs(function, target, layers, fresh):
        def column(t, carry):
            x, y = t // ny, t % ny
            over(function, target, x, y, inside(x, nx), inside(y, ny), layers, fresh)
            return carry

        lax.fori_loop(0, nx * ny, column, 0)

    def side_pairs(function, target, a, b):
        every = (0, 1, 2)
        edge = {-1: 0, 1: None}
        if a and b:
            x, y = (0 if a < 0 else nx - 1), (0 if b < 0 else ny - 1)
            over(function, target, x, y, a + 1, (b + 1, b + 2), every, False)
        elif a:
            x = 0 if a < 0 else nx - 1

            def along_y(y, carry):
                over(function, target, x, y, a + 1, inside(y, ny), every, False)
                return carry

            lax.fori_loop(0, ny, along_y, 0)
        else:
            y = 0 if b < 0 else ny - 1

            def along_x(x, carry):
                over(function, target, x, y, inside(x, nx), (b + 1, b + 2), every, False)
                return carry

            lax.fori_loop(0, nx, along_x, 0)

    def halo_columns(a, b):
        xs = range(1, nx + 1) if a == 0 else [0 if a < 0 else nx + 1]
        ys = range(1, ny + 1) if b == 0 else [0 if b < 0 else ny + 1]
        return [(x, y) for x in xs for y in ys]

    own_columns = halo_columns(0, 0)
    sides = [(-1, 0), (1, 0), (0, -1), (0, 1), (-1, -1), (-1, 1), (1, -1), (1, 1)]

    def start_exchange(buffer, send, recv):
        def source(step, length):
            return (
                pl.ds(length, 1) if step > 0 else pl.ds(1, 1) if step < 0 else pl.ds(1, length)
            )

        def target(step, length):
            return (
                pl.ds(0, 1)
                if step > 0
                else pl.ds(length + 1, 1) if step < 0 else pl.ds(1, length)
            )

        def source_z(step):
            return (
                pl.ds(base + nz - 1, 1)
                if step > 0
                else pl.ds(base, 1) if step < 0 else pl.ds(base, nz)
            )

        def target_z(step):
            return (
                pl.ds(base - 1, 1)
                if step > 0
                else pl.ds(base + nz, 1) if step < 0 else pl.ds(base, nz)
            )

        copies = {}
        for index, direction in enumerate(DIRECTIONS):
            a, b, c = direction
            copy = pltpu.make_async_remote_copy(
                src_ref=buffer.at[source(a, nx), source(b, ny), source_z(c)],
                dst_ref=buffer.at[target(a, nx), target(b, ny), target_z(c)],
                send_sem=send.at[index],
                recv_sem=recv.at[index],
                device_id=peer(direction),
                device_id_type=pl.DeviceIdType.MESH,
            )
            copy.start()
            copies[direction] = copy
        return copies

    def arrive(copies, a, b):
        for c in (0, -1, 1):
            if (a, b, c) != (0, 0, 0):
                copies[(-a, -b, -c)].wait_recv()

    expand([(x, y, 1) for x, y in own_columns])
    for x in range(nx):
        for y in range(ny):
            for k in range(4):
                own[x * ny + y, k : k + 1, :] = jnp.sum(
                    jnp.where(
                        diagonal, spread[x + 1, y + 1, 1, k * slots : (k + 1) * slots, :], 0.0
                    ),
                    axis=0,
                    keepdims=True,
                )
    own_pairs(density, acc, (1,), True)

    pl.semaphore_wait(barrier, len(DIRECTIONS))
    copies = start_exchange(pad, send_sem, recv_sem)
    arrive(copies, 0, 0)
    for x in range(1, nx + 1):
        expand([(x, y, dz) for y in range(1, ny + 1) for dz in (0, 2)])
    own_pairs(density, acc, (0, 2), False)
    for a, b in sides:
        arrive(copies, a, b)
        expand([(x, y, dz) for x, y in halo_columns(a, b) for dz in range(3)])
        side_pairs(density, acc, a, b)

    for t in range(nx * ny):
        for k in range(2):
            rows[k, t : t + 1, :] = jnp.sum(acc[t, k], axis=0, keepdims=True)
        rows[2, t : t + 1, :] = own[t, 3:4, :]
    w = rows[2]
    rho = rows[0] * density_scale - w
    root = jnp.sqrt(jnp.maximum(rho, 0.0) + 1.0)
    big = w > 1.3
    ratio = jnp.where(big, 0.875, jnp.where(w > 0.5, 1.0, 0.0))
    phi_rows[...] = slope_scale * ratio / root
    rows[3] = root

    def fold(line):
        value = jnp.where(cell_mask, jnp.broadcast_to(line, (nz, lanes)), 0.0)
        total = value[:, :WIDE]
        for start in range(WIDE, lanes, WIDE):
            total = total + value[:, start : start + WIDE]
        step = WIDE // 2
        while step >= slots:
            total = total + pltpu.roll(total, step, 1)
            step //= 2
        return total

    for x in range(nx):
        for y in range(ny):
            t = x * ny + y
            line = phi_rows[t : t + 1, :]
            own[t, 4:5, :] = line
            pad_phi[x + 1, y + 1, base : base + nz, :] = fold(line)

    copies_phi = start_exchange(pad_phi, send_phi, recv_phi)

    energy = rows[1] * (energy_scale * w) - 0.25 * w * w
    a_coef = jnp.where(big, 1.4, jnp.where(w > 0.5, 1.0, 0.0))
    rows[3] = energy - a_coef * rows[3]

    expand_phi([(x, y, 1) for x, y in own_columns])
    own_pairs(force, acc_force, (1,), True)
    arrive(copies_phi, 0, 0)
    expand_phi([(x, y, dz) for x, y in own_columns for dz in (0, 2)])
    own_pairs(force, acc_force, (0, 2), False)
    for a, b in sides:
        arrive(copies_phi, a, b)
        expand_phi([(x, y, dz) for x, y in halo_columns(a, b) for dz in range(3)])
        side_pairs(force, acc_force, a, b)

    for x in range(nx):
        for y in range(ny):
            t = x * ny + y
            scale = force_scale * own[t, 3:4, :]
            lines = [
                fold(jnp.sum(acc_force[t, k], axis=0, keepdims=True) * scale) for k in range(3)
            ] + [fold(rows[3, t : t + 1, :])]
            value = lines[3]
            for k in range(3):
                value = jnp.where(group == k, lines[k], value)
            out_ref[x, y] = value

    for direction in DIRECTIONS:
        copies[direction].wait_send()
        copies_phi[direction].wait_send()


def body(axis_sizes, positions, types):
    nx, ny, nz, slots = types.shape
    lanes = nz * slots
    count = len(DIRECTIONS)
    columns = nx * ny
    deep = 16 + nz
    return pl.pallas_call(
        functools.partial(kernel, (nx, ny, nz, slots), axis_sizes),
        out_shape=jax.ShapeDtypeStruct((nx, ny, nz, 4 * slots), jnp.float32),
        in_specs=[pl.BlockSpec(memory_space=pl.ANY), pl.BlockSpec(memory_space=pl.ANY)],
        out_specs=pl.BlockSpec(memory_space=pltpu.VMEM),
        scratch_shapes=[
            pltpu.VMEM((nx, ny, nz, 3 * slots), jnp.float32),
            pltpu.VMEM((nx, ny, nz, slots), jnp.int32),
            pltpu.VMEM((nx + 2, ny + 2, deep, WIDE), jnp.float32),
            pltpu.VMEM((nx + 2, ny + 2, deep, WIDE), jnp.float32),
            pltpu.VMEM((nx + 2, ny + 2, 3, 4 * slots, lanes), jnp.float32),
            pltpu.VMEM((nx + 2, ny + 2, 3, slots, lanes), jnp.float32),
            pltpu.VMEM((columns, 8, lanes), jnp.float32),
            pltpu.VMEM((columns, 2, 8, lanes), jnp.float32),
            pltpu.VMEM((columns, 3, 8, lanes), jnp.float32),
            pltpu.VMEM((4, columns, lanes), jnp.float32),
            pltpu.VMEM((columns, lanes), jnp.float32),
            pltpu.VMEM((3 * nz, lanes), jnp.bfloat16),
            pltpu.VMEM((columns, 9, 3, slots, lanes), jnp.float32),
            pltpu.VMEM((columns, 9, 3, slots, lanes), jnp.float32),
            pltpu.VMEM((columns, 9, 3, slots, lanes), jnp.float32),
            pltpu.SemaphoreType.DMA((2,)),
            pltpu.SemaphoreType.DMA((count,)),
            pltpu.SemaphoreType.DMA((count,)),
            pltpu.SemaphoreType.DMA((count,)),
            pltpu.SemaphoreType.DMA((count,)),
        ],
        compiler_params=pltpu.CompilerParams(
            collective_id=0, has_side_effects=True, vmem_limit_bytes=60 * 1024 * 1024
        ),
    )(positions, types)


def solution(mesh):
    spec = P("gx", "gy", "gz", None)
    sizes = tuple(mesh.shape[axis] for axis in AXES)
    return jax.shard_map(
        functools.partial(body, sizes),
        mesh=mesh,
        in_specs=(spec, spec),
        out_specs=spec,
        check_vma=False,
    )
```

time: 47.5 us -> 28.6 us (0.60)
  Pallas kernels: 44 us -> 27 us
  other arithmetic: 1.49 us -> 0 us
    pallas_call x1, Pallas kernels: 44 us -> 27 us  [body(): pl.pallas_call(functools.partial(kernel, (nx, ny, nz, slots), axis_sizes)...]
    reshape x2 -> x0, local copies, waits for them, and re-layouts: 1.61 us -> none  [the longest x1 0.87 us: body(): out = out.reshape(nx, ny, 4, nz, slots).transpose(0, 1, 3, 2, 4)]
    unnamed x2 -> x1, local copies, waits for them, and re-layouts: 0.01 us -> 1.39 us
    mul x1 -> x0, other arithmetic: 0.78 us -> none  [body(): payload = jnp.concatenate([positions * alpha, weight], axis=3)]
    concatenate x1 -> x0, other arithmetic: 0.7 us -> none  [body(): payload = jnp.concatenate([positions * alpha, weight], axis=3)]
where the time goes in v1:
time: 28.6 us; the launch traced here: 28.4 us
  Pallas kernels  27 us (94%)
  local copies, waits for them, and re-layouts  1.39 us (5%)
    pallas_call x1, Pallas kernels, body(): pl.pallas_call(functools.partial(kernel, (nx, ny, nz, slots), axis_sizes)...  27 us
    unnamed x1, local copies, waits for them, and re-layouts  1.39 us

profile of v1, /device:TPU:0, one launch (start us, length us, event | category | flops | bytes accessed | tf_op | source)
XLA Modules:
  0.0 28.4 jit_solution(2924937616105700580)
XLA Ops:
  0.0 27.0 %shard_map.28 = f32[3,3,8,128]{3,2,1,0:T(8,128)} custom-call(f32[3,3,8,96]{3,2,1,0:T(8,128)} %pos_ref.1, s32[3,3,8,32]{3,2,1,0:T(8,128)} %typ_ref.1), custom_call_target="tpu_custom_call" | custom-call | tf_op jit(solution)/shard_map/pallas_call | solution.py:372
  27.0 1.4 %copy.4 = f32[3,3,8,128]{3,2,1,0:T(8,128)} copy(f32[3,3,8,128]{3,2,1,0:T(8,128)} %shard_map.28) | data formatting | bytes 73728

commit v2 on v1

v2 whole, which is shorter than its diff:
```python
import functools
import math

import jax
import jax.numpy as jnp
from jax import lax
from jax.experimental import pallas as pl
from jax.experimental.pallas import tpu as pltpu
from jax.sharding import PartitionSpec as P

cut_square = 0.9025
density_rate = 3.0
unit = density_rate * math.log2(math.e)
alpha = math.sqrt(unit)
kappa = unit * cut_square
tail = 2.0**-kappa
shift_big = 2.0 * kappa / (cut_square * density_rate)
density_scale = tail / kappa**2
energy_scale = 0.25 * tail**2 / kappa**2
force_scale = -2.0 * tail**2 * density_rate / (kappa**2 * alpha)
slope_scale = -0.5 / tail
far = 1.0e4

AXES = ("gx", "gy", "gz")
DIRECTIONS = sorted(
    (
        (a, b, c)
        for a in (-1, 0, 1)
        for b in (-1, 0, 1)
        for c in (-1, 0, 1)
        if (a, b, c) != (0, 0, 0)
    ),
    key=lambda d: -(2 * abs(d[0]) + 2 * abs(d[1]) + abs(d[2])),
)
SIDES = [(-1, 0), (1, 0), (0, -1), (0, 1), (-1, -1), (-1, 1), (1, -1), (1, 1)]
WIDE = 128
DEEP = 256


def kernel(dims, axis_sizes, pos_ref, typ_ref, out_ref, pos, typ, pad, pad_phi, left, right, moment,
           spread_w, spread_phi, own, acc, acc_force, rows, phi_rows, hot, pair_m, pair_e,
           load_sem, send_sem, recv_sem, send_phi, recv_phi):
    nx, ny, nz, slots = dims
    lanes = nz * slots
    tall = 3 * slots
    base = 8
    f32, bf16 = jnp.float32, jnp.bfloat16
    me = [lax.axis_index(axis) for axis in AXES]

    def peer(direction):
        return {
            axis: lax.rem(place + step + size, size)
            for axis, place, step, size in zip(AXES, me, direction, axis_sizes)
        }

    barrier = pltpu.get_barrier_semaphore()
    for direction in DIRECTIONS:
        pl.semaphore_signal(
            barrier, inc=1, device_id=peer(direction), device_id_type=pl.DeviceIdType.MESH
        )
    loads = [
        pltpu.make_async_copy(pos_ref, pos, load_sem.at[0]),
        pltpu.make_async_copy(typ_ref, typ, load_sem.at[1]),
    ]
    for load in loads:
        load.start()

    cell_mask = (
        lax.broadcasted_iota(jnp.int32, (nz, lanes), 1) // slots
        == lax.broadcasted_iota(jnp.int32, (nz, lanes), 0)
    )
    cells = jnp.where(cell_mask, 1.0, 0.0).astype(f32)
    group = lax.broadcasted_iota(jnp.int32, (nz, WIDE), 1) // slots
    empty = jnp.zeros((nz, lanes), f32)
    full = jnp.ones((nz, WIDE), f32)
    none = jnp.zeros((nz, WIDE), f32)
    parts = DEEP // nz
    used = 27
    hot[...] = jnp.concatenate(
        [empty] * (used - 3) + [cells] * 3 + [empty] * (parts - used), axis=0
    ).astype(bf16)

    for load in loads:
        load.wait()
    for x in range(nx):
        for y in range(ny):
            kind = typ[x, y]
            weight = jnp.where(kind == 1, 1.0, jnp.where(kind == 2, 1.6, 0.0)).astype(f32)
            pad[x + 1, y + 1, base : base + nz, :] = jnp.concatenate(
                [pos[x, y] * alpha, weight], axis=1
            )

    def pieces(value):
        high = value.astype(bf16).astype(f32)
        rest = value - high
        middle = rest.astype(bf16).astype(f32)
        return high, middle, rest - middle

    def choose(values):
        result = values[-1]
        for k in reversed(range(len(values) - 1)):
            result = jnp.where(group == k, values[k], result)
        return result

    def turn(value, step):
        step = (step * slots) % WIDE
        return pltpu.roll(value, step, 1) if step else value

    def centre(k, place):
        return (place - 0.5 * ((nx, ny)[k] + 1) - 0.5) * alpha

    layer = (group.astype(f32) - 1.5) * alpha

    def neighbour(x, y):
        shifted = [pad[x, y, base - 1 + dz : base - 1 + dz + nz, :] for dz in range(3)]
        px, py, pz, w = (
            choose([turn(shifted[dz], dz - q) for dz in range(3)]) for q in range(4)
        )
        px = px + centre(0, x)
        py = py + centre(1, y)
        pz = pz + layer
        square = px * px + py * py + pz * pz
        square = jnp.where(w > 0.0, square, far)
        lines = []
        for value in (px, py, pz):
            h, m, l = pieces(value)
            lines += [h, m, h, l, m, h]
        lines += list(pieces(-square)) + [full] * 3
        ws = list(pieces(w))
        lines += ws + [none] * (parts - used)
        stacked = jnp.concatenate(lines, axis=0).astype(bf16)
        left[x, y] = stacked.T[:tall]
        terms = []
        for value in (w * px, w * py, w * pz):
            terms += list(pieces(value))
        terms = jnp.concatenate(terms + ws, axis=0)
        turned = pltpu.roll(terms, tall, 1)
        lane = lax.broadcasted_iota(jnp.int32, terms.shape, 1)
        moment[x, y, :, :WIDE] = jnp.where(lane < tall, terms, turned).astype(bf16)
        moment[x, y, :, WIDE:] = jnp.where(lane < 2 * tall - WIDE, turned, 0.0).astype(bf16)

    def spread_weight(x, y):
        spread_w[x, y] = jnp.dot(left[x, y], hot[...], preferred_element_type=f32)

    def owner(x, y):
        t = (x - 1) * ny + y - 1
        value = pad[x, y, base : base + nz, :]
        px, py, pz, w = (choose([turn(value, g - q) for g in range(WIDE // slots)]) for q in range(4))
        px = px + centre(0, x)
        py = py + centre(1, y)
        pz = pz - 0.5 * alpha
        square = kappa - (px * px + py * py + pz * pz)

        def tile(value):
            return jnp.where(cell_mask, jnp.concatenate([value] * (lanes // WIDE), axis=1), 0.0)

        lines = []
        for value in (px, py, pz):
            h, m, l = (tile(2.0 * piece) for piece in pieces(value))
            lines += [h, h, m, h, m, l]
        lines += [cells] * 3 + [tile(piece) for piece in pieces(square)]
        lines += [empty] * (parts - used + 3)
        right[t] = jnp.concatenate(lines, axis=0).astype(bf16)
        for k, value in enumerate((px, py, pz, w)):
            own[t, k] = tile(value)
        rows[2, t : t + 1, :] = jnp.sum(own[t, 3], axis=0, keepdims=True)

    def pair(x, y, a, b):
        return (((x - 1) * ny + y - 1) * 3 + a) * 3 + b

    def density(x, y, offsets, fresh):
        t = (x - 1) * ny + y - 1
        zero = jnp.zeros((8, lanes), f32)
        rho, energy = (zero, zero) if fresh else (acc[t, 0], acc[t, 1])
        for a, b in offsets:
            n = pair(x, y, a, b)
            column = (x + a - 1, y + b - 1)
            margin = jnp.dot(left[column], right[t], preferred_element_type=f32)
            for r in range(0, tall, 8):
                m = jnp.maximum(margin[r : r + 8], 0.0)
                e = jnp.exp2(m)
                u = e * m
                q = u * spread_w[column[0], column[1], r : r + 8, :]
                rho = rho + q * m
                energy = energy + q * u
                pair_m[n, r : r + 8, :] = m
                pair_e[n, r : r + 8, :] = e
        acc[t, 0] = rho
        acc[t, 1] = energy

    def slopes(n, carry):
        for r in range(0, tall, 8):
            m = pair_m[n, r : r + 8, :]
            e = pair_e[n, r : r + 8, :]
            u = e * m
            pair_m[n, r : r + 8, :] = u * (m + shift_big)
            pair_e[n, r : r + 8, :] = u * (e * (m + 0.5 * shift_big))
        return carry

    def force(x, y, offsets, fresh):
        t = (x - 1) * ny + y - 1
        phi = jnp.broadcast_to(phi_rows[t : t + 1, :], (slots, lanes))
        total = None
        for a, b in offsets:
            n = pair(x, y, a, b)
            column = (x + a - 1, y + b - 1)
            high, low = [], []
            for r in range(0, tall, slots):
                both = phi + spread_phi[column[0], column[1], r : r + slots, :]
                v = both * pair_m[n, r : r + slots, :] + pair_e[n, r : r + slots, :]
                top = v.astype(bf16)
                high.append(top)
                low.append((v - top.astype(f32)).astype(bf16))
            values = jnp.concatenate(high + low, axis=0)
            part = jnp.dot(
                moment[column[0], column[1], :, : 2 * tall], values, preferred_element_type=f32
            )
            total = part if total is None else total + part
        acc_force[t] = total if fresh else acc_force[t] + total

    def halo_columns(a, b):
        xs = range(1, nx + 1) if a == 0 else [0 if a < 0 else nx + 1]
        ys = range(1, ny + 1) if b == 0 else [0 if b < 0 else ny + 1]
        return [(x, y) for x in xs for y in ys]

    own_columns = halo_columns(0, 0)

    def work(function, columns, fresh):
        for x, y in own_columns:
            offsets = [
                (a, b)
                for a in range(3)
                for b in range(3)
                if (x + a - 1, y + b - 1) in columns
            ]
            if offsets:
                function(x, y, offsets, fresh)

    many = WIDE // slots

    def expand_phi(columns):
        wide = [
            choose(
                [pad_phi[x, y, base - 1 + dz : base - 1 + dz + nz, :] for dz in range(3)]
            )
            for x, y in columns
        ]
        wide = wide[0] if len(wide) == 1 else jnp.concatenate(wide, axis=1)
        stacked = jnp.concatenate(pieces(wide), axis=0).astype(bf16)
        result = lax.dot_general(
            stacked,
            hot[(used - 3) * nz : used * nz, :],
            (((0,), (0,)), ((), ())),
            preferred_element_type=f32,
        )
        for k, (x, y) in enumerate(columns):
            spread_phi[x, y] = result[k * WIDE : k * WIDE + tall]

    def start_exchange(buffer, send, recv):
        def source(step, length):
            return (
                pl.ds(length, 1) if step > 0 else pl.ds(1, 1) if step < 0 else pl.ds(1, length)
            )

        def target(step, length):
            return (
                pl.ds(0, 1)
                if step > 0
                else pl.ds(length + 1, 1) if step < 0 else pl.ds(1, length)
            )

        def source_z(step):
            return (
                pl.ds(base + nz - 1, 1)
                if step > 0
                else pl.ds(base, 1) if step < 0 else pl.ds(base, nz)
            )

        def target_z(step):
            return (
                pl.ds(base - 1, 1)
                if step > 0
                else pl.ds(base + nz, 1) if step < 0 else pl.ds(base, nz)
            )

        copies = {}
        for index, direction in enumerate(DIRECTIONS):
            a, b, c = direction
            copy = pltpu.make_async_remote_copy(
                src_ref=buffer.at[source(a, nx), source(b, ny), source_z(c)],
                dst_ref=buffer.at[target(a, nx), target(b, ny), target_z(c)],
                send_sem=send.at[index],
                recv_sem=recv.at[index],
                device_id=peer(direction),
                device_id_type=pl.DeviceIdType.MESH,
            )
            copy.start()
            copies[direction] = copy
        return copies

    def arrive(copies, a, b):
        for c in (0, -1, 1):
            if (a, b, c) != (0, 0, 0):
                copies[(-a, -b, -c)].wait_recv()

    for x, y in own_columns:
        owner(x, y)

    pl.semaphore_wait(barrier, len(DIRECTIONS))
    copies = start_exchange(pad, send_sem, recv_sem)
    arrive(copies, 0, 0)
    for columns in [own_columns] + SIDES:
        if columns is not own_columns:
            arrive(copies, *columns)
            columns = halo_columns(*columns)
        for x, y in columns:
            neighbour(x, y)
        for x, y in columns:
            spread_weight(x, y)
        work(density, columns, columns is own_columns)

    for t in range(nx * ny):
        for k in range(2):
            rows[k, t : t + 1, :] = jnp.sum(acc[t, k], axis=0, keepdims=True)
    w = rows[2]
    rho = rows[0] * density_scale - w
    root = jnp.sqrt(jnp.maximum(rho, 0.0) + 1.0)
    big = w > 1.3
    ratio = jnp.where(big, 0.875, jnp.where(w > 0.5, 1.0, 0.0))
    phi_rows[...] = slope_scale * ratio / root
    rows[3] = root

    def gather(value):
        total = value[:, :WIDE]
        for start in range(WIDE, lanes, WIDE):
            total = total + value[:, start : start + WIDE]
        step = WIDE // 2
        while step >= slots:
            total = total + pltpu.roll(total, step, 1)
            step //= 2
        return total

    def fold(line):
        return gather(jnp.where(cell_mask, jnp.broadcast_to(line, (nz, lanes)), 0.0))

    for x, y in own_columns:
        t = (x - 1) * ny + y - 1
        pad_phi[x, y, base : base + nz, :] = fold(phi_rows[t : t + 1, :])

    copies_phi = start_exchange(pad_phi, send_phi, recv_phi)

    energy = rows[1] * (energy_scale * w) - 0.25 * w * w
    a_coef = jnp.where(big, 1.4, jnp.where(w > 0.5, 1.0, 0.0))
    rows[3] = energy - a_coef * rows[3]
    lax.fori_loop(0, nx * ny * 9, slopes, 0)

    arrive(copies_phi, 0, 0)
    expand_phi(own_columns)
    work(force, own_columns, True)
    for side in SIDES:
        arrive(copies_phi, *side)
        expand_phi(halo_columns(*side))
        work(force, halo_columns(*side), False)

    for x, y in own_columns:
        t = (x - 1) * ny + y - 1
        sums = [
            acc_force[t, (3 * k) * nz : (3 * k + 1) * nz]
            + acc_force[t, (3 * k + 1) * nz : (3 * k + 2) * nz]
            + acc_force[t, (3 * k + 2) * nz : (3 * k + 3) * nz]
            for k in range(4)
        ]
        scale = force_scale * own[t, 3]
        lines = [gather((sums[k] - own[t, k] * sums[3]) * scale) for k in range(3)]
        out_ref[x - 1, y - 1] = choose(lines + [fold(rows[3, t : t + 1, :])])

    for direction in DIRECTIONS:
        copies[direction].wait_send()
        copies_phi[direction].wait_send()


def body(axis_sizes, positions, types):
    nx, ny, nz, slots = types.shape
    lanes = nz * slots
    tall = 3 * slots
    count = len(DIRECTIONS)
    columns = nx * ny
    deep = 16 + nz
    f32, bf16 = jnp.float32, jnp.bfloat16
    return pl.pallas_call(
        functools.partial(kernel, (nx, ny, nz, slots), axis_sizes),
        out_shape=jax.ShapeDtypeStruct((nx, ny, nz, 4 * slots), f32),
        in_specs=[pl.BlockSpec(memory_space=pl.ANY), pl.BlockSpec(memory_space=pl.ANY)],
        out_specs=pl.BlockSpec(memory_space=pltpu.VMEM),
        scratch_shapes=[
            pltpu.VMEM((nx, ny, nz, 3 * slots), f32),
            pltpu.VMEM((nx, ny, nz, slots), jnp.int32),
            pltpu.VMEM((nx + 2, ny + 2, deep, WIDE), f32),
            pltpu.VMEM((nx + 2, ny + 2, deep, WIDE), f32),
            pltpu.VMEM((nx + 2, ny + 2, tall, DEEP), bf16),
            pltpu.VMEM((columns, DEEP, lanes), bf16),
            pltpu.VMEM((nx + 2, ny + 2, 12 * nz, 2 * WIDE), bf16),
            pltpu.VMEM((nx + 2, ny + 2, tall, lanes), f32),
            pltpu.VMEM((nx + 2, ny + 2, tall, lanes), f32),
            pltpu.VMEM((columns, 4, nz, lanes), f32),
            pltpu.VMEM((columns, 2, 8, lanes), f32),
            pltpu.VMEM((columns, 12 * nz, lanes), f32),
            pltpu.VMEM((4, columns, lanes), f32),
            pltpu.VMEM((columns, lanes), f32),
            pltpu.VMEM((DEEP, lanes), bf16),
            pltpu.VMEM((columns * 9, tall, lanes), f32),
            pltpu.VMEM((columns * 9, tall, lanes), f32),
            pltpu.SemaphoreType.DMA((2,)),
            pltpu.SemaphoreType.DMA((count,)),
            pltpu.SemaphoreType.DMA((count,)),
            pltpu.SemaphoreType.DMA((count,)),
            pltpu.SemaphoreType.DMA((count,)),
        ],
        compiler_params=pltpu.CompilerParams(
            collective_id=0, has_side_effects=True, vmem_limit_bytes=60 * 1024 * 1024
        ),
    )(positions, types)


def solution(mesh):
    spec = P("gx", "gy", "gz", None)
    sizes = tuple(mesh.shape[axis] for axis in AXES)
    return jax.shard_map(
        functools.partial(body, sizes),
        mesh=mesh,
        in_specs=(spec, spec),
        out_specs=spec,
        check_vma=False,
    )
```

time: 28.6 us -> 23.6 us (0.83)
  Pallas kernels: 27 us -> 22 us
    pallas_call x1, Pallas kernels: 27 us -> 22 us  [body(): pl.pallas_call(functools.partial(kernel, (nx, ny, nz, slots), axis_sizes)...]
where the time goes in v2:
time: 23.6 us; the launch traced here: 23.4 us
  Pallas kernels  22 us (93%)
  local copies, waits for them, and re-layouts  1.39 us (6%)
    pallas_call x1, Pallas kernels, body(): pl.pallas_call(functools.partial(kernel, (nx, ny, nz, slots), axis_sizes)...  22 us
    unnamed x1, local copies, waits for them, and re-layouts  1.39 us

profile of v2, /device:TPU:0, one launch (start us, length us, event | category | flops | bytes accessed | tf_op | source)
XLA Modules:
  0.0 23.4 jit_solution(9592539353565638552)
XLA Ops:
  0.0 22.0 %shard_map.28 = f32[3,3,8,128]{3,2,1,0:T(8,128)} custom-call(f32[3,3,8,96]{3,2,1,0:T(8,128)} %pos_ref.1, s32[3,3,8,32]{3,2,1,0:T(8,128)} %typ_ref.1), custom_call_target="tpu_custom_call" | custom-call | tf_op jit(solution)/shard_map/pallas_call | solution.py:390
  22.0 1.4 %copy.4 = f32[3,3,8,128]{3,2,1,0:T(8,128)} copy(f32[3,3,8,128]{3,2,1,0:T(8,128)} %shard_map.28) | data formatting | bytes 73728

commit v3 on v2

--- a/solution.py
+++ b/solution.py
@@ -32,13 +32,16 @@
     ),
     key=lambda d: -(2 * abs(d[0]) + 2 * abs(d[1]) + abs(d[2])),
 )
-SIDES = [(-1, 0), (1, 0), (0, -1), (0, 1), (-1, -1), (-1, 1), (1, -1), (1, 1)]
+BATCHES = [
+    [(-1, 0), (1, 0), (0, -1), (0, 1)],
+    [(-1, -1), (-1, 1), (1, -1), (1, 1)],
+]
 WIDE = 128
 DEEP = 256
 
 
-def kernel(dims, axis_sizes, pos_ref, typ_ref, out_ref, pos, typ, pad, pad_phi, left, right, moment,
-           spread_w, spread_phi, own, acc, acc_force, rows, phi_rows, hot, pair_m, pair_e,
+def kernel(dims, axis_sizes, pos_ref, typ_ref, out_ref, pos, typ, pad, pad_phi, left, left_z, right, moment,
+           spread_w, spread_z, spread_phi, own, acc, acc_force, rows, phi_rows, hot, pair_a, pair_b,
            load_sem, send_sem, recv_sem, send_phi, recv_phi):
     nx, ny, nz, slots = dims
     lanes = nz * slots
@@ -109,18 +112,33 @@
     def centre(k, place):
         return (place - 0.5 * ((nx, ny)[k] + 1) - 0.5) * alpha
 
-    layer = (group.astype(f32) - 1.5) * alpha
-
-    def neighbour(x, y):
-        shifted = [pad[x, y, base - 1 + dz : base - 1 + dz + nz, :] for dz in range(3)]
+    layer = (jnp.minimum(group, 2).astype(f32) - 1.5) * alpha
+
+    cell_row = lax.broadcasted_iota(jnp.int32, (nz, WIDE), 0)
+    outside = ((group == 0) & (cell_row == 0)) | ((group == 2) & (cell_row == nz - 1))
+
+    def neighbour(x, y, part):
+        if part == "inner":
+            middle = pad[x, y, base : base + nz, :]
+            shifted = [
+                jnp.where(cell_row == 0, 0.0, pltpu.roll(middle, 1, 0)),
+                middle,
+                jnp.where(cell_row == nz - 1, 0.0, pltpu.roll(middle, nz - 1, 0)),
+            ]
+        else:
+            shifted = [pad[x, y, base - 1 + dz : base - 1 + dz + nz, :] for dz in range(3)]
+        places = (0, 1, 2, 2)
         px, py, pz, w = (
-            choose([turn(shifted[dz], dz - q) for dz in range(3)]) for q in range(4)
+            choose([turn(shifted[dz], g - q) for g, dz in enumerate(places)]) for q in range(4)
         )
         px = px + centre(0, x)
         py = py + centre(1, y)
         pz = pz + layer
         square = px * px + py * py + pz * pz
-        square = jnp.where(w > 0.0, square, far)
+        present = w > 0.0
+        if part == "outer":
+            present = present & outside
+        square = jnp.where(present, square, far)
         lines = []
         for value in (px, py, pz):
             h, m, l = pieces(value)
@@ -128,19 +146,25 @@
         lines += list(pieces(-square)) + [full] * 3
         ws = list(pieces(w))
         lines += ws + [none] * (parts - used)
-        stacked = jnp.concatenate(lines, axis=0).astype(bf16)
-        left[x, y] = stacked.T[:tall]
-        terms = []
-        for value in (w * px, w * py, w * pz):
-            terms += list(pieces(value))
-        terms = jnp.concatenate(terms + ws, axis=0)
-        turned = pltpu.roll(terms, tall, 1)
-        lane = lax.broadcasted_iota(jnp.int32, terms.shape, 1)
-        moment[x, y, :, :WIDE] = jnp.where(lane < tall, terms, turned).astype(bf16)
-        moment[x, y, :, WIDE:] = jnp.where(lane < 2 * tall - WIDE, turned, 0.0).astype(bf16)
-
-    def spread_weight(x, y):
-        spread_w[x, y] = jnp.dot(left[x, y], hot[...], preferred_element_type=f32)
+        stacked = jnp.concatenate(lines, axis=0).astype(bf16).T
+        if part == "outer":
+            t = (x - 1) * ny + y - 1
+            left_z[t, :slots] = stacked[:slots]
+            left_z[t, slots:] = stacked[2 * slots : tall]
+        else:
+            left[x, y] = stacked[:tall]
+        if part != "inner":
+            terms = []
+            for value in (w * px, w * py, w * pz):
+                terms += list(pieces(value))
+            moment[x, y] = jnp.concatenate(terms + ws, axis=0).astype(bf16)
+
+    def spread_weight(x, y, part):
+        if part == "outer":
+            t = (x - 1) * ny + y - 1
+            spread_z[t] = jnp.dot(left_z[t], hot[...], preferred_element_type=f32)
+        else:
+            spread_w[x, y] = jnp.dot(left[x, y], hot[...], preferred_element_type=f32)
 
     def owner(x, y):
         t = (x - 1) * ny + y - 1
@@ -178,23 +202,42 @@
             margin = jnp.dot(left[column], right[t], preferred_element_type=f32)
             for r in range(0, tall, 8):
                 m = jnp.maximum(margin[r : r + 8], 0.0)
-                e = jnp.exp2(m)
-                u = e * m
+                u = jnp.exp2(m) * m
                 q = u * spread_w[column[0], column[1], r : r + 8, :]
                 rho = rho + q * m
                 energy = energy + q * u
-                pair_m[n, r : r + 8, :] = m
-                pair_e[n, r : r + 8, :] = e
+                pair_a[n, r : r + 8, :] = m
         acc[t, 0] = rho
         acc[t, 1] = energy
 
+    def density_outer(x, y, offsets, fresh):
+        t = (x - 1) * ny + y - 1
+        ends = [(0, 0, slice(0, WIDE)), (slots, 2 * slots, slice(lanes - WIDE, lanes))]
+        sums = [[acc[t, k, :, where] for k in range(2)] for _, _, where in ends]
+        for a, b in offsets:
+            n = pair(x, y, a, b)
+            other = (x + a - 2) * ny + y + b - 2
+            margin = jnp.dot(left_z[other], right[t], preferred_element_type=f32)
+            for (start, place, where), total in zip(ends, sums):
+                for r in range(0, slots, 8):
+                    m = jnp.maximum(margin[start + r : start + r + 8, where], 0.0)
+                    u = jnp.exp2(m) * m
+                    q = u * spread_z[other, start + r : start + r + 8, where]
+                    total[0] = total[0] + q * m
+                    total[1] = total[1] + q * u
+                    rows_at = slice(place + r, place + r + 8)
+                    pair_a[n, rows_at, where] = pair_a[n, rows_at, where] + m
+        for (_, _, where), total in zip(ends, sums):
+            for k in range(2):
+                acc[t, k, :, where] = total[k]
+
     def slopes(n, carry):
         for r in range(0, tall, 8):
-            m = pair_m[n, r : r + 8, :]
-            e = pair_e[n, r : r + 8, :]
+            m = pair_a[n, r : r + 8, :]
+            e = jnp.exp2(m)
             u = e * m
-            pair_m[n, r : r + 8, :] = u * (m + shift_big)
-            pair_e[n, r : r + 8, :] = u * (e * (m + 0.5 * shift_big))
+            pair_a[n, r : r + 8, :] = u * (m + shift_big)
+            pair_b[n, r : r + 8, :] = u * (e * (m + 0.5 * shift_big))
         return carry
 
     def force(x, y, offsets, fresh):
@@ -207,14 +250,14 @@
             high, low = [], []
             for r in range(0, tall, slots):
                 both = phi + spread_phi[column[0], column[1], r : r + slots, :]
-                v = both * pair_m[n, r : r + slots, :] + pair_e[n, r : r + slots, :]
+                v = both * pair_a[n, r : r + slots, :] + pair_b[n, r : r + slots, :]
                 top = v.astype(bf16)
                 high.append(top)
                 low.append((v - top.astype(f32)).astype(bf16))
-            values = jnp.concatenate(high + low, axis=0)
-            part = jnp.dot(
-                moment[column[0], column[1], :, : 2 * tall], values, preferred_element_type=f32
-            )
+            values = jnp.concatenate(high + [low[2], low[0], low[1]], axis=0)
+            terms = moment[column]
+            terms = jnp.concatenate([terms, terms[:, : 2 * slots]], axis=1)
+            part = jnp.dot(terms, values, preferred_element_type=f32)
             total = part if total is None else total + part
         acc_force[t] = total if fresh else acc_force[t] + total
 
@@ -305,19 +348,28 @@
 
     for x, y in own_columns:
         owner(x, y)
+        neighbour(x, y, "inner")
+    for x, y in own_columns:
+        spread_weight(x, y, "inner")
+    work(density, own_columns, True)
 
     pl.semaphore_wait(barrier, len(DIRECTIONS))
     copies = start_exchange(pad, send_sem, recv_sem)
     arrive(copies, 0, 0)
-    for columns in [own_columns] + SIDES:
-        if columns is not own_columns:
-            arrive(copies, *columns)
-            columns = halo_columns(*columns)
+    for x, y in own_columns:
+        neighbour(x, y, "outer")
+    for x, y in own_columns:
+        spread_weight(x, y, "outer")
+    work(density_outer, own_columns, False)
+    for sides in BATCHES:
+        for side in sides:
+            arrive(copies, *side)
+        columns = [column for side in sides for column in halo_columns(*side)]
         for x, y in columns:
-            neighbour(x, y)
+            neighbour(x, y, "all")
         for x, y in columns:
-            spread_weight(x, y)
-        work(density, columns, columns is own_columns)
+            spread_weight(x, y, "all")
+        work(density, columns, False)
 
     for t in range(nx * ny):
         for k in range(2):
@@ -357,10 +409,12 @@
     arrive(copies_phi, 0, 0)
     expand_phi(own_columns)
     work(force, own_columns, True)
-    for side in SIDES:
-        arrive(copies_phi, *side)
-        expand_phi(halo_columns(*side))
-        work(force, halo_columns(*side), False)
+    for sides in BATCHES:
+        for side in sides:
+            arrive(copies_phi, *side)
+        columns = [column for side in sides for column in halo_columns(*side)]
+        expand_phi(columns)
+        work(force, columns, False)
 
     for x, y in own_columns:
         t = (x - 1) * ny + y - 1
@@ -389,7 +443,7 @@
     f32, bf16 = jnp.float32, jnp.bfloat16
     return pl.pallas_call(
         functools.partial(kernel, (nx, ny, nz, slots), axis_sizes),
-        out_shape=jax.ShapeDtypeStruct((nx, ny, nz, 4 * slots), f32),
+        out_shape=pltpu.VMEM((nx, ny, nz, 4 * slots), f32),
         in_specs=[pl.BlockSpec(memory_space=pl.ANY), pl.BlockSpec(memory_space=pl.ANY)],
         out_specs=pl.BlockSpec(memory_space=pltpu.VMEM),
         scratch_shapes=[
@@ -398,9 +452,11 @@
             pltpu.VMEM((nx + 2, ny + 2, deep, WIDE), f32),
             pltpu.VMEM((nx + 2, ny + 2, deep, WIDE), f32),
             pltpu.VMEM((nx + 2, ny + 2, tall, DEEP), bf16),
+            pltpu.VMEM((columns, 2 * slots, DEEP), bf16),
             pltpu.VMEM((columns, DEEP, lanes), bf16),
-            pltpu.VMEM((nx + 2, ny + 2, 12 * nz, 2 * WIDE), bf16),
+            pltpu.VMEM((nx + 2, ny + 2, 12 * nz, WIDE), bf16),
             pltpu.VMEM((nx + 2, ny + 2, tall, lanes), f32),
+            pltpu.VMEM((columns, 2 * slots, lanes), f32),
             pltpu.VMEM((nx + 2, ny + 2, tall, lanes), f32),
             pltpu.VMEM((columns, 4, nz, lanes), f32),
             pltpu.VMEM((columns, 2, 8, lanes), f32),

time: 23.6 us -> 20.6 us (0.87)
  Pallas kernels: 22 us -> 19.8 us
  local copies, waits for them, and re-layouts: 1.39 us -> 0.62 us
    pallas_call x1, Pallas kernels: 22 us -> 19.8 us  [body(): pl.pallas_call(functools.partial(kernel, (nx, ny, nz, slots), axis_sizes)...]
    unnamed x1, local copies, waits for them, and re-layouts: 1.39 us -> 0.62 us
where the time goes in v3:
time: 20.6 us; the launch traced here: 20.4 us
  Pallas kernels  19.8 us (96%)
  local copies, waits for them, and re-layouts  0.62 us (3%)
    pallas_call x1, Pallas kernels, body(): pl.pallas_call(functools.partial(kernel, (nx, ny, nz, slots), axis_sizes)...  19.8 us
    unnamed x1, local copies, waits for them, and re-layouts  0.62 us

profile of v3, /device:TPU:0, one launch (start us, length us, event | category | flops | bytes accessed | tf_op | source)
XLA Modules:
  0.0 20.4 jit_solution(14620053969166950716)
XLA Ops:
  0.0 19.8 %shard_map.28 = f32[3,3,8,128]{3,2,1,0:T(8,128)S(1)} custom-call(f32[3,3,8,96]{3,2,1,0:T(8,128)} %pos_ref.1, s32[3,3,8,32]{3,2,1,0:T(8,128)} %typ_ref.1), custom_call_target="tpu_custom_call" | custom-call | tf_op jit(solution)/shard_map/pallas_call | solution.py:444
  19.8 0.6 %copy.4 = f32[3,3,8,128]{3,2,1,0:T(8,128)} copy(f32[3,3,8,128]{3,2,1,0:T(8,128)S(1)} %shard_map.28) | data formatting | bytes 73728

commit v4 on v3

--- a/solution.py
+++ b/solution.py
@@ -32,17 +32,21 @@
     ),
     key=lambda d: -(2 * abs(d[0]) + 2 * abs(d[1]) + abs(d[2])),
 )
-BATCHES = [
-    [(-1, 0), (1, 0), (0, -1), (0, 1)],
-    [(-1, -1), (-1, 1), (1, -1), (1, 1)],
-]
+SIDES = [(-1, 0), (1, 0), (0, -1), (0, 1)]
+CORNERS = [(-1, -1), (-1, 1), (1, -1), (1, 1)]
+
+
+def stage(direction):
+    return abs(direction[0]) + abs(direction[1])
+
+
 WIDE = 128
 DEEP = 256
 
 
 def kernel(dims, axis_sizes, pos_ref, typ_ref, out_ref, pos, typ, pad, pad_phi, left, left_z, right, moment,
            spread_w, spread_z, spread_phi, own, acc, acc_force, rows, phi_rows, hot, pair_a, pair_b,
-           load_sem, send_sem, recv_sem, send_phi, recv_phi):
+           blank, load_sem, send_sem, recv_sem, recv_phi):
     nx, ny, nz, slots = dims
     lanes = nz * slots
     tall = 3 * slots
@@ -231,14 +235,13 @@
             for k in range(2):
                 acc[t, k, :, where] = total[k]
 
-    def slopes(n, carry):
+    def slopes(n):
         for r in range(0, tall, 8):
             m = pair_a[n, r : r + 8, :]
             e = jnp.exp2(m)
             u = e * m
             pair_a[n, r : r + 8, :] = u * (m + shift_big)
             pair_b[n, r : r + 8, :] = u * (e * (m + 0.5 * shift_big))
-        return carry
 
     def force(x, y, offsets, fresh):
         t = (x - 1) * ny + y - 1
@@ -250,7 +253,12 @@
             high, low = [], []
             for r in range(0, tall, slots):
                 both = phi + spread_phi[column[0], column[1], r : r + slots, :]
-                v = both * pair_a[n, r : r + slots, :] + pair_b[n, r : r + slots, :]
+                if fresh:
+                    m = pair_a[n, r : r + slots, :]
+                    e = jnp.exp2(m)
+                    v = (e * m) * (both * (m + shift_big) + e * (m + 0.5 * shift_big))
+                else:
+                    v = both * pair_a[n, r : r + slots, :] + pair_b[n, r : r + slots, :]
                 top = v.astype(bf16)
                 high.append(top)
                 low.append((v - top.astype(f32)).astype(bf16))
@@ -267,6 +275,8 @@
         return [(x, y) for x in xs for y in ys]
 
     own_columns = halo_columns(0, 0)
+    side_columns = [column for side in SIDES for column in halo_columns(*side)]
+    corner_columns = [column for side in CORNERS for column in halo_columns(*side)]
 
     def work(function, columns, fresh):
         for x, y in own_columns:
@@ -326,50 +336,50 @@
                 else pl.ds(base + nz, 1) if step < 0 else pl.ds(base, nz)
             )
 
-        copies = {}
-        for index, direction in enumerate(DIRECTIONS):
+        for direction in DIRECTIONS:
             a, b, c = direction
-            copy = pltpu.make_async_remote_copy(
+            pltpu.make_async_remote_copy(
                 src_ref=buffer.at[source(a, nx), source(b, ny), source_z(c)],
                 dst_ref=buffer.at[target(a, nx), target(b, ny), target_z(c)],
-                send_sem=send.at[index],
-                recv_sem=recv.at[index],
+                send_sem=send,
+                recv_sem=recv.at[stage(direction)],
                 device_id=peer(direction),
                 device_id_type=pl.DeviceIdType.MESH,
-            )
-            copy.start()
-            copies[direction] = copy
-        return copies
-
-    def arrive(copies, a, b):
-        for c in (0, -1, 1):
-            if (a, b, c) != (0, 0, 0):
-                copies[(-a, -b, -c)].wait_recv()
+            ).start()
+
+    def await_rows(directions, semaphore):
+        count = sum(
+            (1 if a else nx) * (1 if b else ny) * (1 if c else nz) for a, b, c in directions
+        )
+        part = blank.at[pl.ds(0, count)]
+        pltpu.make_async_copy(part, part, semaphore).wait()
+
+    def arrive(recv, number):
+        await_rows([d for d in DIRECTIONS if stage(d) == number], recv.at[number])
 
     for x, y in own_columns:
         owner(x, y)
         neighbour(x, y, "inner")
     for x, y in own_columns:
         spread_weight(x, y, "inner")
+
+    pl.semaphore_wait(barrier, len(DIRECTIONS))
+    start_exchange(pad, send_sem.at[0], recv_sem)
     work(density, own_columns, True)
-
-    pl.semaphore_wait(barrier, len(DIRECTIONS))
-    copies = start_exchange(pad, send_sem, recv_sem)
-    arrive(copies, 0, 0)
+    arrive(recv_sem, 0)
     for x, y in own_columns:
         neighbour(x, y, "outer")
     for x, y in own_columns:
         spread_weight(x, y, "outer")
     work(density_outer, own_columns, False)
-    for sides in BATCHES:
-        for side in sides:
-            arrive(copies, *side)
-        columns = [column for side in sides for column in halo_columns(*side)]
-        for x, y in columns:
-            neighbour(x, y, "all")
-        for x, y in columns:
-            spread_weight(x, y, "all")
-        work(density, columns, False)
+    arrive(recv_sem, 1)
+    arrive(recv_sem, 2)
+    columns = side_columns + corner_columns
+    for x, y in columns:
+        neighbour(x, y, "all")
+    for x, y in columns:
+        spread_weight(x, y, "all")
+    work(density, columns, False)
 
     for t in range(nx * ny):
         for k in range(2):
@@ -399,22 +409,26 @@
         t = (x - 1) * ny + y - 1
         pad_phi[x, y, base : base + nz, :] = fold(phi_rows[t : t + 1, :])
 
-    copies_phi = start_exchange(pad_phi, send_phi, recv_phi)
+    start_exchange(pad_phi, send_sem.at[1], recv_phi)
 
     energy = rows[1] * (energy_scale * w) - 0.25 * w * w
     a_coef = jnp.where(big, 1.4, jnp.where(w > 0.5, 1.0, 0.0))
     rows[3] = energy - a_coef * rows[3]
-    lax.fori_loop(0, nx * ny * 9, slopes, 0)
-
-    arrive(copies_phi, 0, 0)
+    for x, y in own_columns:
+        for a in range(3):
+            for b in range(3):
+                if (x + a - 1, y + b - 1) not in own_columns:
+                    slopes(pair(x, y, a, b))
+
+    arrive(recv_phi, 0)
     expand_phi(own_columns)
     work(force, own_columns, True)
-    for sides in BATCHES:
-        for side in sides:
-            arrive(copies_phi, *side)
-        columns = [column for side in sides for column in halo_columns(*side)]
-        expand_phi(columns)
-        work(force, columns, False)
+    arrive(recv_phi, 1)
+    expand_phi(side_columns)
+    work(force, side_columns, False)
+    arrive(recv_phi, 2)
+    expand_phi(corner_columns)
+    work(force, corner_columns, False)
 
     for x, y in own_columns:
         t = (x - 1) * ny + y - 1
@@ -428,16 +442,14 @@
         lines = [gather((sums[k] - own[t, k] * sums[3]) * scale) for k in range(3)]
         out_ref[x - 1, y - 1] = choose(lines + [fold(rows[3, t : t + 1, :])])
 
-    for direction in DIRECTIONS:
-        copies[direction].wait_send()
-        copies_phi[direction].wait_send()
+    for number in range(2):
+        await_rows(DIRECTIONS, send_sem.at[number])
 
 
 def body(axis_sizes, positions, types):
     nx, ny, nz, slots = types.shape
     lanes = nz * slots
     tall = 3 * slots
-    count = len(DIRECTIONS)
     columns = nx * ny
     deep = 16 + nz
     f32, bf16 = jnp.float32, jnp.bfloat16
@@ -466,11 +478,11 @@
             pltpu.VMEM((DEEP, lanes), bf16),
             pltpu.VMEM((columns * 9, tall, lanes), f32),
             pltpu.VMEM((columns * 9, tall, lanes), f32),
+            pltpu.VMEM(((nx + 2) * (ny + 2) * nz, WIDE), f32),
             pltpu.SemaphoreType.DMA((2,)),
-            pltpu.SemaphoreType.DMA((count,)),
-            pltpu.SemaphoreType.DMA((count,)),
-            pltpu.SemaphoreType.DMA((count,)),
-            pltpu.SemaphoreType.DMA((count,)),
+            pltpu.SemaphoreType.DMA((2,)),
+            pltpu.SemaphoreType.DMA((3,)),
+            pltpu.SemaphoreType.DMA((3,)),
         ],
         compiler_params=pltpu.CompilerParams(
             collective_id=0, has_side_effects=True, vmem_limit_bytes=60 * 1024 * 1024

time: 20.6 us -> 21.2 us (1.029)
  Pallas kernels: 19.8 us -> 20.4 us
    pallas_call x1, Pallas kernels: 19.8 us -> 20.4 us  [body(): pl.pallas_call(functools.partial(kernel, (nx, ny, nz, slots), axis_sizes)...]
where the time goes in v4:
time: 21.2 us; the launch traced here: 21 us
  Pallas kernels  20.4 us (96%)
  local copies, waits for them, and re-layouts  0.62 us (3%)
    pallas_call x1, Pallas kernels, body(): pl.pallas_call(functools.partial(kernel, (nx, ny, nz, slots), axis_sizes)...  20.4 us
    unnamed x1, local copies, waits for them, and re-layouts  0.62 us

profile of v4, /device:TPU:0, one launch (start us, length us, event | category | flops | bytes accessed | tf_op | source)
XLA Modules:
  0.0 21.0 jit_solution(3009433605489730123)
XLA Ops:
  0.0 20.4 %shard_map.28 = f32[3,3,8,128]{3,2,1,0:T(8,128)S(1)} custom-call(f32[3,3,8,96]{3,2,1,0:T(8,128)} %pos_ref.1, s32[3,3,8,32]{3,2,1,0:T(8,128)} %typ_ref.1), custom_call_target="tpu_custom_call" | custom-call | tf_op jit(solution)/shard_map/pallas_call | solution.py:456
  20.4 0.6 %copy.4 = f32[3,3,8,128]{3,2,1,0:T(8,128)} copy(f32[3,3,8,128]{3,2,1,0:T(8,128)S(1)} %shard_map.28) | data formatting | bytes 73728

commit v5 on v4

--- a/solution.py
+++ b/solution.py
@@ -357,29 +357,46 @@
     def arrive(recv, number):
         await_rows([d for d in DIRECTIONS if stage(d) == number], recv.at[number])
 
+    always = me[0] >= 0
+    early = (me[0] + 1) // 2 + me[1] < 3
+
+    def region(condition):
+        return lambda function: pl.when(condition)(function)
+
     for x, y in own_columns:
         owner(x, y)
-        neighbour(x, y, "inner")
-    for x, y in own_columns:
-        spread_weight(x, y, "inner")
-
+
+    def own_inner():
+        for x, y in own_columns:
+            neighbour(x, y, "inner")
+        for x, y in own_columns:
+            spread_weight(x, y, "inner")
+        work(density, own_columns, True)
+
+    region(early)(own_inner)
     pl.semaphore_wait(barrier, len(DIRECTIONS))
     start_exchange(pad, send_sem.at[0], recv_sem)
-    work(density, own_columns, True)
-    arrive(recv_sem, 0)
-    for x, y in own_columns:
-        neighbour(x, y, "outer")
-    for x, y in own_columns:
-        spread_weight(x, y, "outer")
-    work(density_outer, own_columns, False)
-    arrive(recv_sem, 1)
-    arrive(recv_sem, 2)
-    columns = side_columns + corner_columns
-    for x, y in columns:
-        neighbour(x, y, "all")
-    for x, y in columns:
-        spread_weight(x, y, "all")
-    work(density, columns, False)
+    region(jnp.logical_not(early))(own_inner)
+
+    @region(always)
+    def own_outer():
+        arrive(recv_sem, 0)
+        for x, y in own_columns:
+            neighbour(x, y, "outer")
+        for x, y in own_columns:
+            spread_weight(x, y, "outer")
+        work(density_outer, own_columns, False)
+
+    @region(always)
+    def halo():
+        arrive(recv_sem, 1)
+        arrive(recv_sem, 2)
+        columns = side_columns + corner_columns
+        for x, y in columns:
+            neighbour(x, y, "all")
+        for x, y in columns:
+            spread_weight(x, y, "all")
+        work(density, columns, False)
 
     for t in range(nx * ny):
         for k in range(2):
@@ -411,21 +428,30 @@
 
     start_exchange(pad_phi, send_sem.at[1], recv_phi)
 
-    energy = rows[1] * (energy_scale * w) - 0.25 * w * w
-    a_coef = jnp.where(big, 1.4, jnp.where(w > 0.5, 1.0, 0.0))
-    rows[3] = energy - a_coef * rows[3]
-    for x, y in own_columns:
-        for a in range(3):
-            for b in range(3):
-                if (x + a - 1, y + b - 1) not in own_columns:
-                    slopes(pair(x, y, a, b))
-
-    arrive(recv_phi, 0)
-    expand_phi(own_columns)
-    work(force, own_columns, True)
-    arrive(recv_phi, 1)
-    expand_phi(side_columns)
-    work(force, side_columns, False)
+    @region(always)
+    def between():
+        w = rows[2]
+        energy = rows[1] * (energy_scale * w) - 0.25 * w * w
+        a_coef = jnp.where(w > 1.3, 1.4, jnp.where(w > 0.5, 1.0, 0.0))
+        rows[3] = energy - a_coef * rows[3]
+        for x, y in own_columns:
+            for a in range(3):
+                for b in range(3):
+                    if (x + a - 1, y + b - 1) not in own_columns:
+                        slopes(pair(x, y, a, b))
+
+    @region(always)
+    def own_force():
+        arrive(recv_phi, 0)
+        expand_phi(own_columns)
+        work(force, own_columns, True)
+
+    @region(always)
+    def side_force():
+        arrive(recv_phi, 1)
+        expand_phi(side_columns)
+        work(force, side_columns, False)
+
     arrive(recv_phi, 2)
     expand_phi(corner_columns)
     work(force, corner_columns, False)

time: 21.2 us -> 19.4 us (0.915)
  Pallas kernels: 20.4 us -> 18.6 us
    pallas_call x1, Pallas kernels: 20.4 us -> 18.6 us  [body(): pl.pallas_call(functools.partial(kernel, (nx, ny, nz, slots), axis_sizes)...]
where the time goes in v5:
time: 19.4 us; the launch traced here: 19.3 us
  Pallas kernels  18.6 us (96%)
  local copies, waits for them, and re-layouts  0.62 us (3%)
    pallas_call x1, Pallas kernels, body(): pl.pallas_call(functools.partial(kernel, (nx, ny, nz, slots), axis_sizes)...  18.6 us
    unnamed x1, local copies, waits for them, and re-layouts  0.62 us

profile of v5, /device:TPU:0, one launch (start us, length us, event | category | flops | bytes accessed | tf_op | source)
XLA Modules:
  0.0 19.3 jit_solution(18432580704625413096)
XLA Ops:
  0.0 18.6 %shard_map.28 = f32[3,3,8,128]{3,2,1,0:T(8,128)S(1)} custom-call(f32[3,3,8,96]{3,2,1,0:T(8,128)} %pos_ref.1, s32[3,3,8,32]{3,2,1,0:T(8,128)} %typ_ref.1), custom_call_target="tpu_custom_call" | custom-call | tf_op jit(solution)/shard_map/pallas_call | solution.py:482
  18.6 0.6 %copy.4 = f32[3,3,8,128]{3,2,1,0:T(8,128)} copy(f32[3,3,8,128]{3,2,1,0:T(8,128)S(1)} %shard_map.28) | data formatting | bytes 73728

commit v6 on v5

--- a/solution.py
+++ b/solution.py
@@ -32,12 +32,13 @@
     ),
     key=lambda d: -(2 * abs(d[0]) + 2 * abs(d[1]) + abs(d[2])),
 )
-SIDES = [(-1, 0), (1, 0), (0, -1), (0, 1)]
+X_SIDES = [(-1, 0), (1, 0)]
+Y_SIDES = [(0, -1), (0, 1)]
 CORNERS = [(-1, -1), (-1, 1), (1, -1), (1, 1)]
 
 
 def stage(direction):
-    return abs(direction[0]) + abs(direction[1])
+    return abs(direction[0]) + 2 * abs(direction[1])
 
 
 WIDE = 128
@@ -275,8 +276,12 @@
         return [(x, y) for x in xs for y in ys]
 
     own_columns = halo_columns(0, 0)
-    side_columns = [column for side in SIDES for column in halo_columns(*side)]
-    corner_columns = [column for side in CORNERS for column in halo_columns(*side)]
+    x_columns, y_columns, corner_columns = (
+        [column for side in sides for column in halo_columns(*side)]
+        for sides in (X_SIDES, Y_SIDES, CORNERS)
+    )
+    last = [(x, y) for x in sorted({1, nx}) for y in sorted({1, ny})]
+    first = [column for column in own_columns if column not in last]
 
     def work(function, columns, fresh):
         for x, y in own_columns:
@@ -387,28 +392,6 @@
             spread_weight(x, y, "outer")
         work(density_outer, own_columns, False)
 
-    @region(always)
-    def halo():
-        arrive(recv_sem, 1)
-        arrive(recv_sem, 2)
-        columns = side_columns + corner_columns
-        for x, y in columns:
-            neighbour(x, y, "all")
-        for x, y in columns:
-            spread_weight(x, y, "all")
-        work(density, columns, False)
-
-    for t in range(nx * ny):
-        for k in range(2):
-            rows[k, t : t + 1, :] = jnp.sum(acc[t, k], axis=0, keepdims=True)
-    w = rows[2]
-    rho = rows[0] * density_scale - w
-    root = jnp.sqrt(jnp.maximum(rho, 0.0) + 1.0)
-    big = w > 1.3
-    ratio = jnp.where(big, 0.875, jnp.where(w > 0.5, 1.0, 0.0))
-    phi_rows[...] = slope_scale * ratio / root
-    rows[3] = root
-
     def gather(value):
         total = value[:, :WIDE]
         for start in range(WIDE, lanes, WIDE):
@@ -422,9 +405,44 @@
     def fold(line):
         return gather(jnp.where(cell_mask, jnp.broadcast_to(line, (nz, lanes)), 0.0))
 
-    for x, y in own_columns:
-        t = (x - 1) * ny + y - 1
-        pad_phi[x, y, base : base + nz, :] = fold(phi_rows[t : t + 1, :])
+    def halo(number, columns):
+        arrive(recv_sem, number)
+        for x, y in columns:
+            neighbour(x, y, "all")
+        for x, y in columns:
+            spread_weight(x, y, "all")
+        work(density, columns, False)
+
+    def derivatives(columns):
+        places = [(x - 1) * ny + y - 1 for x, y in columns]
+        for t in places:
+            for k in range(2):
+                rows[k, t : t + 1, :] = jnp.sum(acc[t, k], axis=0, keepdims=True)
+        rho, w = (
+            jnp.concatenate([rows[k, t : t + 1, :] for t in places], axis=0) for k in (0, 2)
+        )
+        root = jnp.sqrt(jnp.maximum(rho * density_scale - w, 0.0) + 1.0)
+        ratio = jnp.where(w > 1.3, 0.875, jnp.where(w > 0.5, 1.0, 0.0))
+        phi = slope_scale * ratio / root
+        for k, (t, (x, y)) in enumerate(zip(places, columns)):
+            line = phi[k : k + 1]
+            pad_phi[x, y, base : base + nz, :] = fold(line)
+            phi_rows[t : t + 1, :] = line
+            rows[3, t : t + 1, :] = root[k : k + 1]
+
+    @region(always)
+    def halo_x():
+        halo(1, x_columns)
+
+    @region(always)
+    def halo_y():
+        halo(2, y_columns)
+        derivatives(first)
+
+    @region(always)
+    def halo_corners():
+        halo(3, corner_columns)
+        derivatives(last)
 
     start_exchange(pad_phi, send_sem.at[1], recv_phi)
 
@@ -446,27 +464,35 @@
         expand_phi(own_columns)
         work(force, own_columns, True)
 
-    @region(always)
-    def side_force():
-        arrive(recv_phi, 1)
-        expand_phi(side_columns)
-        work(force, side_columns, False)
-
-    arrive(recv_phi, 2)
-    expand_phi(corner_columns)
-    work(force, corner_columns, False)
-
-    for x, y in own_columns:
-        t = (x - 1) * ny + y - 1
-        sums = [
-            acc_force[t, (3 * k) * nz : (3 * k + 1) * nz]
-            + acc_force[t, (3 * k + 1) * nz : (3 * k + 2) * nz]
-            + acc_force[t, (3 * k + 2) * nz : (3 * k + 3) * nz]
-            for k in range(4)
-        ]
-        scale = force_scale * own[t, 3]
-        lines = [gather((sums[k] - own[t, k] * sums[3]) * scale) for k in range(3)]
-        out_ref[x - 1, y - 1] = choose(lines + [fold(rows[3, t : t + 1, :])])
+    def halo_force(number, columns):
+        arrive(recv_phi, number)
+        expand_phi(columns)
+        work(force, columns, False)
+
+    def write(columns):
+        for x, y in columns:
+            t = (x - 1) * ny + y - 1
+            sums = [
+                acc_force[t, (3 * k) * nz : (3 * k + 1) * nz]
+                + acc_force[t, (3 * k + 1) * nz : (3 * k + 2) * nz]
+                + acc_force[t, (3 * k + 2) * nz : (3 * k + 3) * nz]
+                for k in range(4)
+            ]
+            scale = force_scale * own[t, 3]
+            lines = [gather((sums[k] - own[t, k] * sums[3]) * scale) for k in range(3)]
+            out_ref[x - 1, y - 1] = choose(lines + [fold(rows[3, t : t + 1, :])])
+
+    @region(always)
+    def force_x():
+        halo_force(1, x_columns)
+
+    @region(always)
+    def force_y():
+        halo_force(2, y_columns)
+        write(first)
+
+    halo_force(3, corner_columns)
+    write(last)
 
     for number in range(2):
         await_rows(DIRECTIONS, send_sem.at[number])
@@ -507,8 +533,8 @@
             pltpu.VMEM(((nx + 2) * (ny + 2) * nz, WIDE), f32),
             pltpu.SemaphoreType.DMA((2,)),
             pltpu.SemaphoreType.DMA((2,)),
-            pltpu.SemaphoreType.DMA((3,)),
-            pltpu.SemaphoreType.DMA((3,)),
+            pltpu.SemaphoreType.DMA((4,)),
+            pltpu.SemaphoreType.DMA((4,)),
         ],
         compiler_params=pltpu.CompilerParams(
             collective_id=0, has_side_effects=True, vmem_limit_bytes=60 * 1024 * 1024

time: 19.4 us -> 19 us (0.979)
  Pallas kernels: 18.6 us -> 18.2 us
    pallas_call x1, Pallas kernels: 18.6 us -> 18.2 us  [body(): pl.pallas_call(functools.partial(kernel, (nx, ny, nz, slots), axis_sizes)...]
where the time goes in v6:
time: 19 us; the launch traced here: 18.9 us
  Pallas kernels  18.2 us (96%)
  local copies, waits for them, and re-layouts  0.62 us (3%)
    pallas_call x1, Pallas kernels, body(): pl.pallas_call(functools.partial(kernel, (nx, ny, nz, slots), axis_sizes)...  18.2 us
    unnamed x1, local copies, waits for them, and re-layouts  0.62 us

profile of v6, /device:TPU:0, one launch (start us, length us, event | category | flops | bytes accessed | tf_op | source)
XLA Modules:
  0.0 18.9 jit_solution(16879648031522689411)
XLA Ops:
  0.0 18.2 %shard_map.28 = f32[3,3,8,128]{3,2,1,0:T(8,128)S(1)} custom-call(f32[3,3,8,96]{3,2,1,0:T(8,128)} %pos_ref.1, s32[3,3,8,32]{3,2,1,0:T(8,128)} %typ_ref.1), custom_call_target="tpu_custom_call" | custom-call | tf_op jit(solution)/shard_map/pallas_call | solution.py:508
  18.2 0.6 %copy.4 = f32[3,3,8,128]{3,2,1,0:T(8,128)} copy(f32[3,3,8,128]{3,2,1,0:T(8,128)S(1)} %shard_map.28) | data formatting | bytes 73728

commit v7 on v6

--- a/solution.py
+++ b/solution.py
@@ -32,13 +32,9 @@
     ),
     key=lambda d: -(2 * abs(d[0]) + 2 * abs(d[1]) + abs(d[2])),
 )
-X_SIDES = [(-1, 0), (1, 0)]
-Y_SIDES = [(0, -1), (0, 1)]
-CORNERS = [(-1, -1), (-1, 1), (1, -1), (1, 1)]
-
-
 def stage(direction):
-    return abs(direction[0]) + 2 * abs(direction[1])
+    a, b, _ = direction
+    return 2 + (b > 0) if b else abs(a)
 
 
 WIDE = 128
@@ -46,7 +42,7 @@
 
 
 def kernel(dims, axis_sizes, pos_ref, typ_ref, out_ref, pos, typ, pad, pad_phi, left, left_z, right, moment,
-           spread_w, spread_z, spread_phi, own, acc, acc_force, rows, phi_rows, hot, pair_a, pair_b,
+           moment_phi, weighted, spread_w, spread_z, spread_phi, own, acc, acc_force, rows, phi_rows, hot, pair_a, pair_s,
            blank, load_sem, send_sem, recv_sem, recv_phi):
     nx, ny, nz, slots = dims
     lanes = nz * slots
@@ -115,7 +111,7 @@
         return pltpu.roll(value, step, 1) if step else value
 
     def centre(k, place):
-        return (place - 0.5 * ((nx, ny)[k] + 1) - 0.5) * alpha
+        return (jnp.asarray(place, f32) - (0.5 * ((nx, ny)[k] + 1) + 0.5)) * alpha
 
     layer = (jnp.minimum(group, 2).astype(f32) - 1.5) * alpha
 
@@ -159,9 +155,12 @@
         else:
             left[x, y] = stacked[:tall]
         if part != "inner":
+            values = (w * px, w * py, w * pz)
             terms = []
-            for value in (w * px, w * py, w * pz):
+            for k, value in enumerate(values):
                 terms += list(pieces(value))
+                weighted[x, y, k] = value
+            weighted[x, y, 3] = w
             moment[x, y] = jnp.concatenate(terms + ws, axis=0).astype(bf16)
 
     def spread_weight(x, y, part):
@@ -192,19 +191,33 @@
         right[t] = jnp.concatenate(lines, axis=0).astype(bf16)
         for k, value in enumerate((px, py, pz, w)):
             own[t, k] = tile(value)
-        rows[2, t : t + 1, :] = jnp.sum(own[t, 3], axis=0, keepdims=True)
+        rows[2, t] = jnp.sum(own[t, 3], axis=0, keepdims=True)
 
     def pair(x, y, a, b):
         return (((x - 1) * ny + y - 1) * 3 + a) * 3 + b
+
+    def margins(operands, t):
+        step = 3
+        for start in range(0, len(operands), step):
+            part = operands[start : start + step]
+            height = part[0].shape[0]
+            product = jnp.dot(
+                part[0] if len(part) == 1 else jnp.concatenate(part, axis=0),
+                right[t],
+                preferred_element_type=f32,
+            )
+            for k in range(len(part)):
+                yield product[k * height : (k + 1) * height]
 
     def density(x, y, offsets, fresh):
         t = (x - 1) * ny + y - 1
         zero = jnp.zeros((8, lanes), f32)
         rho, energy = (zero, zero) if fresh else (acc[t, 0], acc[t, 1])
-        for a, b in offsets:
+        columns = [(x + a - 1, y + b - 1) for a, b in offsets]
+        for (a, b), column, margin in zip(
+            offsets, columns, margins([left[column] for column in columns], t)
+        ):
             n = pair(x, y, a, b)
-            column = (x + a - 1, y + b - 1)
-            margin = jnp.dot(left[column], right[t], preferred_element_type=f32)
             for r in range(0, tall, 8):
                 m = jnp.maximum(margin[r : r + 8], 0.0)
                 u = jnp.exp2(m) * m
@@ -219,10 +232,11 @@
         t = (x - 1) * ny + y - 1
         ends = [(0, 0, slice(0, WIDE)), (slots, 2 * slots, slice(lanes - WIDE, lanes))]
         sums = [[acc[t, k, :, where] for k in range(2)] for _, _, where in ends]
-        for a, b in offsets:
+        others = [(x + a - 2) * ny + y + b - 2 for a, b in offsets]
+        for (a, b), other, margin in zip(
+            offsets, others, margins([left_z[other] for other in others], t)
+        ):
             n = pair(x, y, a, b)
-            other = (x + a - 2) * ny + y + b - 2
-            margin = jnp.dot(left_z[other], right[t], preferred_element_type=f32)
             for (start, place, where), total in zip(ends, sums):
                 for r in range(0, slots, 8):
                     m = jnp.maximum(margin[start + r : start + r + 8, where], 0.0)
@@ -236,39 +250,72 @@
             for k in range(2):
                 acc[t, k, :, where] = total[k]
 
-    def slopes(n):
-        for r in range(0, tall, 8):
-            m = pair_a[n, r : r + 8, :]
-            e = jnp.exp2(m)
-            u = e * m
-            pair_a[n, r : r + 8, :] = u * (m + shift_big)
-            pair_b[n, r : r + 8, :] = u * (e * (m + 0.5 * shift_big))
+    def twice(terms):
+        return jnp.concatenate([terms, terms[:, : 2 * slots]], axis=1)
+
+    def split(value):
+        high = value.astype(bf16)
+        return high, (value - high.astype(f32)).astype(bf16)
+
+    def stack(layers):
+        high, low = zip(*layers)
+        return jnp.concatenate(list(high) + [low[2], low[0], low[1]], axis=0)
+
+    def product(left_terms, values):
+        return jnp.dot(twice(left_terms), values, preferred_element_type=f32)
 
     def force(x, y, offsets, fresh):
         t = (x - 1) * ny + y - 1
-        phi = jnp.broadcast_to(phi_rows[t : t + 1, :], (slots, lanes))
+        phi = jnp.broadcast_to(phi_rows[t], (slots, lanes))
         total = None
         for a, b in offsets:
             n = pair(x, y, a, b)
             column = (x + a - 1, y + b - 1)
-            high, low = [], []
+            layers = []
             for r in range(0, tall, slots):
+                m = pair_a[n, r : r + slots, :]
+                e = jnp.exp2(m)
                 both = phi + spread_phi[column[0], column[1], r : r + slots, :]
-                if fresh:
-                    m = pair_a[n, r : r + slots, :]
-                    e = jnp.exp2(m)
-                    v = (e * m) * (both * (m + shift_big) + e * (m + 0.5 * shift_big))
-                else:
-                    v = both * pair_a[n, r : r + slots, :] + pair_b[n, r : r + slots, :]
-                top = v.astype(bf16)
-                high.append(top)
-                low.append((v - top.astype(f32)).astype(bf16))
-            values = jnp.concatenate(high + [low[2], low[0], low[1]], axis=0)
-            terms = moment[column]
-            terms = jnp.concatenate([terms, terms[:, : 2 * slots]], axis=1)
-            part = jnp.dot(terms, values, preferred_element_type=f32)
+                v = (e * m) * (both * (m + shift_big) + e * (m + 0.5 * shift_big))
+                layers.append(split(v))
+            part = product(moment[column], stack(layers))
             total = part if total is None else total + part
         acc_force[t] = total if fresh else acc_force[t] + total
+
+    def force_fixed(x, y, offsets, fresh):
+        t = (x - 1) * ny + y - 1
+        phi = jnp.broadcast_to(phi_rows[t], (slots, lanes))
+        total = None
+        for a, b in offsets:
+            n = pair(x, y, a, b)
+            fixed, slope = [], []
+            for r in range(0, tall, slots):
+                m = pair_a[n, r : r + slots, :]
+                e = jnp.exp2(m)
+                u = e * m
+                value = u * (m + shift_big)
+                fixed.append(split(phi * value + u * (e * (m + 0.5 * shift_big))))
+                slope.append(split(value))
+            pair_s[n] = stack(slope)
+            part = product(moment[x + a - 1, y + b - 1], stack(fixed))
+            total = part if total is None else total + part
+        acc_force[t] = total if fresh else acc_force[t] + total
+
+    def force_remote(x, y, offsets, fresh):
+        t = (x - 1) * ny + y - 1
+        total = None
+        for a, b in offsets:
+            part = product(moment_phi[x + a - 1, y + b - 1], pair_s[pair(x, y, a, b)])
+            total = part if total is None else total + part
+        acc_force[t] = acc_force[t] + total
+
+    def derivative_terms(x, y):
+        shifted = [pad_phi[x, y, base - 1 + dz : base - 1 + dz + nz, :] for dz in (0, 1, 2, 2)]
+        phi = choose(shifted)
+        terms = []
+        for k in range(4):
+            terms += list(pieces(phi * weighted[x, y, k]))
+        moment_phi[x, y] = jnp.concatenate(terms, axis=0).astype(bf16)
 
     def halo_columns(a, b):
         xs = range(1, nx + 1) if a == 0 else [0 if a < 0 else nx + 1]
@@ -276,12 +323,19 @@
         return [(x, y) for x in xs for y in ys]
 
     own_columns = halo_columns(0, 0)
-    x_columns, y_columns, corner_columns = (
-        [column for side in sides for column in halo_columns(*side)]
-        for sides in (X_SIDES, Y_SIDES, CORNERS)
-    )
-    last = [(x, y) for x in sorted({1, nx}) for y in sorted({1, ny})]
-    first = [column for column in own_columns if column not in last]
+    x_columns = halo_columns(-1, 0) + halo_columns(1, 0)
+    all_halo = [
+        (x, y) for x in range(nx + 2) for y in range(ny + 2) if (x, y) not in own_columns
+    ]
+
+    def around(x, y):
+        return [(x + a, y + b) for a in (-1, 0, 1) for b in (-1, 0, 1)]
+
+    far_row = jnp.where(2 * me[1] >= axis_sizes[1], 1, 0)
+    near_row = 1 - far_row
+
+    def row_of(side):
+        return 1 + (ny - 1) * side, (ny + 1) * side
 
     def work(function, columns, fresh):
         for x, y in own_columns:
@@ -293,8 +347,6 @@
             ]
             if offsets:
                 function(x, y, offsets, fresh)
-
-    many = WIDE // slots
 
     def expand_phi(columns):
         wide = [
@@ -360,10 +412,11 @@
         pltpu.make_async_copy(part, part, semaphore).wait()
 
     def arrive(recv, number):
-        await_rows([d for d in DIRECTIONS if stage(d) == number], recv.at[number])
+        kind = number if isinstance(number, int) else 2
+        await_rows([d for d in DIRECTIONS if stage(d) == kind], recv.at[number])
 
     always = me[0] >= 0
-    early = (me[0] + 1) // 2 + me[1] < 3
+    early = (me[0] + 1) // 2 + me[1] < 2
 
     def region(condition):
         return lambda function: pl.when(condition)(function)
@@ -405,44 +458,61 @@
     def fold(line):
         return gather(jnp.where(cell_mask, jnp.broadcast_to(line, (nz, lanes)), 0.0))
 
-    def halo(number, columns):
-        arrive(recv_sem, number)
-        for x, y in columns:
+    def halo_x():
+        arrive(recv_sem, 1)
+        for x, y in x_columns:
             neighbour(x, y, "all")
-        for x, y in columns:
+        for x, y in x_columns:
             spread_weight(x, y, "all")
-        work(density, columns, False)
+        work(density, x_columns, False)
+
+    def row_work(function, side):
+        y = row_of(side)[0]
+        for x in range(1, nx + 1):
+            function(x, y, [(a, 2 * side) for a in range(3)], False)
+
+    def halo_row(side):
+        arrive(recv_sem, 3 - side)
+        y = row_of(side)[1]
+        for x in range(nx + 2):
+            neighbour(x, y, "all")
+        for x in range(nx + 2):
+            spread_weight(x, y, "all")
+        row_work(density, side)
+
+    def row_columns(*sides):
+        return [(x, row_of(side)[0]) for x in range(1, nx + 1) for side in sides]
+
+    middle_columns = [(x, y) for x in range(1, nx + 1) for y in range(2, ny)]
 
     def derivatives(columns):
         places = [(x - 1) * ny + y - 1 for x, y in columns]
         for t in places:
             for k in range(2):
-                rows[k, t : t + 1, :] = jnp.sum(acc[t, k], axis=0, keepdims=True)
-        rho, w = (
-            jnp.concatenate([rows[k, t : t + 1, :] for t in places], axis=0) for k in (0, 2)
-        )
+                rows[k, t] = jnp.sum(acc[t, k], axis=0, keepdims=True)
+        rho, w = (jnp.concatenate([rows[k, t] for t in places], axis=0) for k in (0, 2))
         root = jnp.sqrt(jnp.maximum(rho * density_scale - w, 0.0) + 1.0)
         ratio = jnp.where(w > 1.3, 0.875, jnp.where(w > 0.5, 1.0, 0.0))
         phi = slope_scale * ratio / root
         for k, (t, (x, y)) in enumerate(zip(places, columns)):
             line = phi[k : k + 1]
             pad_phi[x, y, base : base + nz, :] = fold(line)
-            phi_rows[t : t + 1, :] = line
-            rows[3, t : t + 1, :] = root[k : k + 1]
-
-    @region(always)
-    def halo_x():
-        halo(1, x_columns)
-
-    @region(always)
-    def halo_y():
-        halo(2, y_columns)
-        derivatives(first)
-
-    @region(always)
-    def halo_corners():
-        halo(3, corner_columns)
-        derivatives(last)
+            phi_rows[t] = line
+            rows[3, t] = root[k : k + 1]
+
+    @region(always)
+    def halo_near():
+        halo_row(near_row)
+
+    @region(always)
+    def halo_sides():
+        halo_x()
+        derivatives(middle_columns + row_columns(near_row))
+
+    @region(always)
+    def halo_far():
+        halo_row(far_row)
+        derivatives(row_columns(far_row))
 
     start_exchange(pad_phi, send_sem.at[1], recv_phi)
 
@@ -452,22 +522,21 @@
         energy = rows[1] * (energy_scale * w) - 0.25 * w * w
         a_coef = jnp.where(w > 1.3, 1.4, jnp.where(w > 0.5, 1.0, 0.0))
         rows[3] = energy - a_coef * rows[3]
-        for x, y in own_columns:
-            for a in range(3):
-                for b in range(3):
-                    if (x + a - 1, y + b - 1) not in own_columns:
-                        slopes(pair(x, y, a, b))
+        work(force_fixed, all_halo, True)
 
     @region(always)
     def own_force():
         arrive(recv_phi, 0)
         expand_phi(own_columns)
-        work(force, own_columns, True)
-
-    def halo_force(number, columns):
-        arrive(recv_phi, number)
-        expand_phi(columns)
-        work(force, columns, False)
+        for x, y in own_columns:
+            inner = all(column in own_columns for column in around(x, y))
+            offsets = [
+                (a, b)
+                for a in range(3)
+                for b in range(3)
+                if (x + a - 1, y + b - 1) in own_columns
+            ]
+            force(x, y, offsets, inner)
 
     def write(columns):
         for x, y in columns:
@@ -480,19 +549,30 @@
             ]
             scale = force_scale * own[t, 3]
             lines = [gather((sums[k] - own[t, k] * sums[3]) * scale) for k in range(3)]
-            out_ref[x - 1, y - 1] = choose(lines + [fold(rows[3, t : t + 1, :])])
-
-    @region(always)
-    def force_x():
-        halo_force(1, x_columns)
-
-    @region(always)
-    def force_y():
-        halo_force(2, y_columns)
-        write(first)
-
-    halo_force(3, corner_columns)
-    write(last)
+            out_ref[x - 1, y - 1] = choose(lines + [fold(rows[3, t])])
+
+    def force_row(side):
+        arrive(recv_phi, 3 - side)
+        for x in range(nx + 2):
+            derivative_terms(x, row_of(side)[1])
+        row_work(force_remote, side)
+
+    @region(always)
+    def force_near():
+        force_row(near_row)
+
+    @region(always)
+    def force_sides():
+        arrive(recv_phi, 1)
+        for x, y in x_columns:
+            derivative_terms(x, y)
+        work(force_remote, x_columns, False)
+        write(middle_columns + row_columns(near_row))
+
+    @region(always)
+    def force_far():
+        force_row(far_row)
+        write(row_columns(far_row))
 
     for number in range(2):
         await_rows(DIRECTIONS, send_sem.at[number])
@@ -519,17 +599,19 @@
             pltpu.VMEM((columns, 2 * slots, DEEP), bf16),
             pltpu.VMEM((columns, DEEP, lanes), bf16),
             pltpu.VMEM((nx + 2, ny + 2, 12 * nz, WIDE), bf16),
+            pltpu.VMEM((nx + 2, ny + 2, 12 * nz, WIDE), bf16),
+            pltpu.VMEM((nx + 2, ny + 2, 4, nz, WIDE), f32),
             pltpu.VMEM((nx + 2, ny + 2, tall, lanes), f32),
             pltpu.VMEM((columns, 2 * slots, lanes), f32),
             pltpu.VMEM((nx + 2, ny + 2, tall, lanes), f32),
             pltpu.VMEM((columns, 4, nz, lanes), f32),
             pltpu.VMEM((columns, 2, 8, lanes), f32),
             pltpu.VMEM((columns, 12 * nz, lanes), f32),
-            pltpu.VMEM((4, columns, lanes), f32),
-            pltpu.VMEM((columns, lanes), f32),
+            pltpu.VMEM((4, columns, 1, lanes), f32),
+            pltpu.VMEM((columns, 1, lanes), f32),
             pltpu.VMEM((DEEP, lanes), bf16),
             pltpu.VMEM((columns * 9, tall, lanes), f32),
-            pltpu.VMEM((columns * 9, tall, lanes), f32),
+            pltpu.VMEM((columns * 9, 2 * tall, lanes), bf16),
             pltpu.VMEM(((nx + 2) * (ny + 2) * nz, WIDE), f32),
             pltpu.SemaphoreType.DMA((2,)),
             pltpu.SemaphoreType.DMA((2,)),

time: 19 us -> 18.3 us (0.963)
  Pallas kernels: 18.2 us -> 17.5 us
    pallas_call x1, Pallas kernels: 18.2 us -> 17.5 us  [body(): pl.pallas_call(functools.partial(kernel, (nx, ny, nz, slots), axis_sizes)...]
where the time goes in v7:
time: 18.3 us; the launch traced here: 18.1 us
  Pallas kernels  17.5 us (96%)
  local copies, waits for them, and re-layouts  0.62 us (3%)
    pallas_call x1, Pallas kernels, body(): pl.pallas_call(functools.partial(kernel, (nx, ny, nz, slots), axis_sizes)...  17.5 us
    unnamed x1, local copies, waits for them, and re-layouts  0.62 us

profile of v7, /device:TPU:0, one launch (start us, length us, event | category | flops | bytes accessed | tf_op | source)
XLA Modules:
  0.0 18.1 jit_solution(5860507340758078113)
XLA Ops:
  0.0 17.5 %shard_map.28 = f32[3,3,8,128]{3,2,1,0:T(8,128)S(1)} custom-call(f32[3,3,8,96]{3,2,1,0:T(8,128)} %pos_ref.1, s32[3,3,8,32]{3,2,1,0:T(8,128)} %typ_ref.1), custom_call_target="tpu_custom_call" | custom-call | tf_op jit(solution)/shard_map/pallas_call | solution.py:588
  17.5 0.6 %copy.4 = f32[3,3,8,128]{3,2,1,0:T(8,128)} copy(f32[3,3,8,128]{3,2,1,0:T(8,128)S(1)} %shard_map.28) | data formatting | bytes 73728

commit v8 on v7

--- a/solution.py
+++ b/solution.py
@@ -42,7 +42,7 @@
 
 
 def kernel(dims, axis_sizes, pos_ref, typ_ref, out_ref, pos, typ, pad, pad_phi, left, left_z, right, moment,
-           moment_phi, weighted, spread_w, spread_z, spread_phi, own, acc, acc_force, rows, phi_rows, hot, pair_a, pair_s,
+           moment_phi, weighted, spread_w, spread_z, spread_phi, own, acc, acc_force, rows, phi_rows, hot, pair_a, pair_b, pair_s,
            blank, load_sem, send_sem, recv_sem, recv_phi):
     nx, ny, nz, slots = dims
     lanes = nz * slots
@@ -163,12 +163,23 @@
             weighted[x, y, 3] = w
             moment[x, y] = jnp.concatenate(terms + ws, axis=0).astype(bf16)
 
-    def spread_weight(x, y, part):
-        if part == "outer":
-            t = (x - 1) * ny + y - 1
-            spread_z[t] = jnp.dot(left_z[t], hot[...], preferred_element_type=f32)
-        else:
-            spread_w[x, y] = jnp.dot(left[x, y], hot[...], preferred_element_type=f32)
+    def spread_weights(columns, part):
+        step = 3
+        for start in range(0, len(columns), step):
+            some = columns[start : start + step]
+            if part == "outer":
+                places = [((x - 1) * ny + y - 1,) for x, y in some]
+                source, target = left_z, spread_z
+            else:
+                places, source, target = some, left, spread_w
+            height = source.shape[-2]
+            result = jnp.dot(
+                jnp.concatenate([source[place] for place in places], axis=0),
+                hot[...],
+                preferred_element_type=f32,
+            )
+            for k, place in enumerate(places):
+                target[place] = result[k * height : (k + 1) * height]
 
     def owner(x, y):
         t = (x - 1) * ny + y - 1
@@ -209,10 +220,13 @@
             for k in range(len(part)):
                 yield product[k * height : (k + 1) * height]
 
+    def slopes(m, e, u):
+        return u * (m + shift_big), u * (e * (m + 0.5 * shift_big))
+
     def density(x, y, offsets, fresh):
         t = (x - 1) * ny + y - 1
         zero = jnp.zeros((8, lanes), f32)
-        rho, energy = (zero, zero) if fresh else (acc[t, 0], acc[t, 1])
+        rho, energy = (zero, zero) if fresh else (acc[t, 0], None)
         columns = [(x + a - 1, y + b - 1) for a, b in offsets]
         for (a, b), column, margin in zip(
             offsets, columns, margins([left[column] for column in columns], t)
@@ -220,13 +234,18 @@
             n = pair(x, y, a, b)
             for r in range(0, tall, 8):
                 m = jnp.maximum(margin[r : r + 8], 0.0)
-                u = jnp.exp2(m) * m
+                e = jnp.exp2(m)
+                u = e * m
                 q = u * spread_w[column[0], column[1], r : r + 8, :]
                 rho = rho + q * m
-                energy = energy + q * u
-                pair_a[n, r : r + 8, :] = m
+                if fresh:
+                    energy = energy + q * u
+                    pair_a[n, r : r + 8, :], pair_b[n, r : r + 8, :] = slopes(m, e, u)
+                else:
+                    pair_a[n, r : r + 8, :] = m
         acc[t, 0] = rho
-        acc[t, 1] = energy
+        if fresh:
+            acc[t, 1] = energy
 
     def density_outer(x, y, offsets, fresh):
         t = (x - 1) * ny + y - 1
@@ -240,12 +259,15 @@
             for (start, place, where), total in zip(ends, sums):
                 for r in range(0, slots, 8):
                     m = jnp.maximum(margin[start + r : start + r + 8, where], 0.0)
-                    u = jnp.exp2(m) * m
+                    e = jnp.exp2(m)
+                    u = e * m
                     q = u * spread_z[other, start + r : start + r + 8, where]
                     total[0] = total[0] + q * m
                     total[1] = total[1] + q * u
                     rows_at = slice(place + r, place + r + 8)
-                    pair_a[n, rows_at, where] = pair_a[n, rows_at, where] + m
+                    slope_a, slope_b = slopes(m, e, u)
+                    pair_a[n, rows_at, where] = pair_a[n, rows_at, where] + slope_a
+                    pair_b[n, rows_at, where] = pair_b[n, rows_at, where] + slope_b
         for (_, _, where), total in zip(ends, sums):
             for k in range(2):
                 acc[t, k, :, where] = total[k]
@@ -273,10 +295,8 @@
             column = (x + a - 1, y + b - 1)
             layers = []
             for r in range(0, tall, slots):
-                m = pair_a[n, r : r + slots, :]
-                e = jnp.exp2(m)
                 both = phi + spread_phi[column[0], column[1], r : r + slots, :]
-                v = (e * m) * (both * (m + shift_big) + e * (m + 0.5 * shift_big))
+                v = both * pair_a[n, r : r + slots, :] + pair_b[n, r : r + slots, :]
                 layers.append(split(v))
             part = product(moment[column], stack(layers))
             total = part if total is None else total + part
@@ -285,21 +305,26 @@
     def force_fixed(x, y, offsets, fresh):
         t = (x - 1) * ny + y - 1
         phi = jnp.broadcast_to(phi_rows[t], (slots, lanes))
-        total = None
+        total, energy = None, acc[t, 1]
         for a, b in offsets:
             n = pair(x, y, a, b)
+            column = (x + a - 1, y + b - 1)
             fixed, slope = [], []
             for r in range(0, tall, slots):
                 m = pair_a[n, r : r + slots, :]
                 e = jnp.exp2(m)
                 u = e * m
-                value = u * (m + shift_big)
-                fixed.append(split(phi * value + u * (e * (m + 0.5 * shift_big))))
-                slope.append(split(value))
+                quotas = u * u * spread_w[column[0], column[1], r : r + slots, :]
+                for k in range(0, slots, 8):
+                    energy = energy + quotas[k : k + 8]
+                slope_a, slope_b = slopes(m, e, u)
+                fixed.append(split(phi * slope_a + slope_b))
+                slope.append(split(slope_a))
             pair_s[n] = stack(slope)
-            part = product(moment[x + a - 1, y + b - 1], stack(fixed))
+            part = product(moment[column], stack(fixed))
             total = part if total is None else total + part
         acc_force[t] = total if fresh else acc_force[t] + total
+        acc[t, 1] = energy
 
     def force_remote(x, y, offsets, fresh):
         t = (x - 1) * ny + y - 1
@@ -427,8 +452,7 @@
     def own_inner():
         for x, y in own_columns:
             neighbour(x, y, "inner")
-        for x, y in own_columns:
-            spread_weight(x, y, "inner")
+        spread_weights(own_columns, "inner")
         work(density, own_columns, True)
 
     region(early)(own_inner)
@@ -441,8 +465,7 @@
         arrive(recv_sem, 0)
         for x, y in own_columns:
             neighbour(x, y, "outer")
-        for x, y in own_columns:
-            spread_weight(x, y, "outer")
+        spread_weights(own_columns, "outer")
         work(density_outer, own_columns, False)
 
     def gather(value):
@@ -462,8 +485,7 @@
         arrive(recv_sem, 1)
         for x, y in x_columns:
             neighbour(x, y, "all")
-        for x, y in x_columns:
-            spread_weight(x, y, "all")
+        spread_weights(x_columns, "all")
         work(density, x_columns, False)
 
     def row_work(function, side):
@@ -476,8 +498,7 @@
         y = row_of(side)[1]
         for x in range(nx + 2):
             neighbour(x, y, "all")
-        for x in range(nx + 2):
-            spread_weight(x, y, "all")
+        spread_weights([(x, y) for x in range(nx + 2)], "all")
         row_work(density, side)
 
     def row_columns(*sides):
@@ -488,17 +509,15 @@
     def derivatives(columns):
         places = [(x - 1) * ny + y - 1 for x, y in columns]
         for t in places:
-            for k in range(2):
-                rows[k, t] = jnp.sum(acc[t, k], axis=0, keepdims=True)
+            rows[0, t] = jnp.sum(acc[t, 0], axis=0, keepdims=True)
         rho, w = (jnp.concatenate([rows[k, t] for t in places], axis=0) for k in (0, 2))
-        root = jnp.sqrt(jnp.maximum(rho * density_scale - w, 0.0) + 1.0)
+        inverse = lax.rsqrt(jnp.maximum(rho * density_scale - w, 0.0) + 1.0)
         ratio = jnp.where(w > 1.3, 0.875, jnp.where(w > 0.5, 1.0, 0.0))
-        phi = slope_scale * ratio / root
+        phi = slope_scale * ratio * inverse
         for k, (t, (x, y)) in enumerate(zip(places, columns)):
             line = phi[k : k + 1]
             pad_phi[x, y, base : base + nz, :] = fold(line)
             phi_rows[t] = line
-            rows[3, t] = root[k : k + 1]
 
     @region(always)
     def halo_near():
@@ -518,11 +537,15 @@
 
     @region(always)
     def between():
+        work(force_fixed, all_halo, True)
+        for t in range(nx * ny):
+            rows[1, t] = jnp.sum(acc[t, 1], axis=0, keepdims=True)
         w = rows[2]
         energy = rows[1] * (energy_scale * w) - 0.25 * w * w
         a_coef = jnp.where(w > 1.3, 1.4, jnp.where(w > 0.5, 1.0, 0.0))
-        rows[3] = energy - a_coef * rows[3]
-        work(force_fixed, all_halo, True)
+        occupied = jnp.maximum(rows[0] * density_scale - w, 0.0) + 1.0
+        rows[3] = energy - a_coef * jnp.sqrt(occupied)
+
 
     @region(always)
     def own_force():
@@ -611,6 +634,7 @@
             pltpu.VMEM((columns, 1, lanes), f32),
             pltpu.VMEM((DEEP, lanes), bf16),
             pltpu.VMEM((columns * 9, tall, lanes), f32),
+            pltpu.VMEM((columns * 9, tall, lanes), f32),
             pltpu.VMEM((columns * 9, 2 * tall, lanes), bf16),
             pltpu.VMEM(((nx + 2) * (ny + 2) * nz, WIDE), f32),
             pltpu.SemaphoreType.DMA((2,)),

time: 18.3 us -> 18.1 us (0.989)
  Pallas kernels: 17.5 us -> 17.3 us
    pallas_call x1, Pallas kernels: 17.5 us -> 17.3 us  [body(): pl.pallas_call(functools.partial(kernel, (nx, ny, nz, slots), axis_sizes)...]
where the time goes in v8:
time: 18.1 us; the launch traced here: 17.9 us
  Pallas kernels  17.3 us (96%)
  local copies, waits for them, and re-layouts  0.62 us (3%)
    pallas_call x1, Pallas kernels, body(): pl.pallas_call(functools.partial(kernel, (nx, ny, nz, slots), axis_sizes)...  17.3 us
    unnamed x1, local copies, waits for them, and re-layouts  0.62 us

profile of v8, /device:TPU:0, one launch (start us, length us, event | category | flops | bytes accessed | tf_op | source)
XLA Modules:
  0.0 17.9 jit_solution(1905966268206301068)
XLA Ops:
  0.0 17.3 %shard_map.28 = f32[3,3,8,128]{3,2,1,0:T(8,128)S(1)} custom-call(f32[3,3,8,96]{3,2,1,0:T(8,128)} %pos_ref.1, s32[3,3,8,32]{3,2,1,0:T(8,128)} %typ_ref.1), custom_call_target="tpu_custom_call" | custom-call | tf_op jit(solution)/shard_map/pallas_call | solution.py:611
  17.3 0.6 %copy.4 = f32[3,3,8,128]{3,2,1,0:T(8,128)} copy(f32[3,3,8,128]{3,2,1,0:T(8,128)S(1)} %shard_map.28) | data formatting | bytes 73728

commit v9 on v8

--- a/solution.py
+++ b/solution.py
@@ -155,13 +155,17 @@
         else:
             left[x, y] = stacked[:tall]
         if part != "inner":
-            values = (w * px, w * py, w * pz)
-            terms = []
-            for k, value in enumerate(values):
-                terms += list(pieces(value))
+            for k, value in enumerate((px, py, pz, w)):
                 weighted[x, y, k] = value
-            weighted[x, y, 3] = w
-            moment[x, y] = jnp.concatenate(terms + ws, axis=0).astype(bf16)
+
+    def moments(x, y):
+        w = weighted[x, y, 3]
+        terms = []
+        for k in range(3):
+            value = w * weighted[x, y, k]
+            weighted[x, y, k] = value
+            terms += list(pieces(value))
+        moment[x, y] = jnp.concatenate(terms + list(pieces(w)), axis=0).astype(bf16)
 
     def spread_weights(columns, part):
         step = 3
@@ -537,6 +541,8 @@
 
     @region(always)
     def between():
+        for x, y in all_halo + own_columns:
+            moments(x, y)
         work(force_fixed, all_halo, True)
         for t in range(nx * ny):
             rows[1, t] = jnp.sum(acc[t, 1], axis=0, keepdims=True)

time: 18.1 us -> 18.1 us (level)
  no operation moved by 1% of the time
where the time goes in v9:
time: 18.1 us; the launch traced here: 17.9 us
  Pallas kernels  17.3 us (96%)
  local copies, waits for them, and re-layouts  0.62 us (3%)
    pallas_call x1, Pallas kernels, body(): pl.pallas_call(functools.partial(kernel, (nx, ny, nz, slots), axis_sizes)...  17.3 us
    unnamed x1, local copies, waits for them, and re-layouts  0.62 us

profile of v9, /device:TPU:0, one launch (start us, length us, event | category | flops | bytes accessed | tf_op | source)
XLA Modules:
  0.0 17.9 jit_solution(10176707535116156404)
XLA Ops:
  0.0 17.3 %shard_map.28 = f32[3,3,8,128]{3,2,1,0:T(8,128)S(1)} custom-call(f32[3,3,8,96]{3,2,1,0:T(8,128)} %pos_ref.1, s32[3,3,8,32]{3,2,1,0:T(8,128)} %typ_ref.1), custom_call_target="tpu_custom_call" | custom-call | tf_op jit(solution)/shard_map/pallas_call | solution.py:617
  17.3 0.6 %copy.4 = f32[3,3,8,128]{3,2,1,0:T(8,128)} copy(f32[3,3,8,128]{3,2,1,0:T(8,128)S(1)} %shard_map.28) | data formatting | bytes 73728
